TPU v7x, 256 devices: a whole 4x4x8 slice. The times are simulated.
256 devices in a mesh: rep: 8 (over z_lo, x), pts: 32 (over y, z_hi, core).
Axes of the slice: x: 4, y: 4, z: 8 (z_hi: 4, z_lo: 2; z = z_hi * 2 + z_lo), core: 2. Of those that a mesh axis runs over, the one named last changes fastest.
Arguments:
- fine_points: bfloat16 [262144, 256], P(('rep', 'pts')), may hold values from -6 to 6
- parent: int32 [262144], P(('rep', 'pts')), may hold values from 0 to 65535, as said below
- patch_count: int32 [256], P(('rep', 'pts')), may hold values from 512 to 1024
- qkv_fine: bfloat16 [256, 768], replicated, may hold values from -0.375 to 0.375
- out_fine: bfloat16 [256, 256], replicated, may hold values from -0.375 to 0.375
- pool_weight: bfloat16 [256, 512], replicated, may hold values from -0.375 to 0.375
- qkv_coarse: bfloat16 [512, 1536], replicated, may hold values from -0.25 to 0.25
- out_coarse: bfloat16 [512, 512], replicated, may hold values from -0.25 to 0.25
- cotangent: bfloat16 [65536, 512], P(('rep', 'pts')), may hold values from -6 to 6
Outputs:
- coarse_out: bfloat16 [65536, 512], P(('rep', 'pts'))
- grad_out_fine: bfloat16 [256, 256], replicated
- grad_pool: bfloat16 [256, 512], replicated
- grad_qkv_coarse: bfloat16 [512, 1536], replicated
- grad_out_coarse: bfloat16 [512, 512], replicated
Inputs may be any that keep to these rules, and one draw needn't show every extreme that they name: `parent`: along the points of block b, parents never fall and lie in pooled rows b * 256 to (b + 1) * 256 + 31; the last block of each replica (pts index 31) keeps its parents in its own 256 rows.
All inputs are finite; a program needn't handle non-finite values.
Results may differ from a plain program's by a relative error of at most 0.018.
Values may be sent and summed in bfloat16 or wider, within the bound.
A program may use at most 128 MiB of HBM per device.

v0:
```python
import jax
import jax.numpy as jnp
from jax import lax
from jax.sharding import PartitionSpec as P

HD = 16
PATCH = 1024
Q_DEV = 256
SPILL = 32


epsilon = 1e-06
logit_scale = 0.25


def from_behind(block, axis, distance):
    devices = range(lax.axis_size(axis))
    route = [(i - distance, i) for i in devices if i - distance in devices]
    return lax.ppermute(block, axis, route)


def swapped(value, axis, apart):
    mask = 2**apart
    pairs = [(source, source ^ mask) for source in range(lax.axis_size(axis))]
    return lax.ppermute(value, axis, pairs)


def split_up(shard, dim, peers):
    before, after = (shard.shape[:dim], shard.shape[dim + 1 :])
    return jnp.moveaxis(shard.reshape(*before, peers, -1, *after), dim, 0)


def sum_together(arrays, axis, dims):
    peers = lax.axis_size(axis)
    pieces = [split_up(a, dim, peers) for a, dim in zip(arrays, dims)]
    lines = jnp.concatenate([b.reshape(peers, -1) for b in pieces], axis=1)
    span = max(16, -(-lines.shape[1] // 1024) * 8)
    lines = jnp.pad(lines, ((0, 0), (0, span * 128 - lines.shape[1]))).reshape(-1, 128)
    vector, at, finished = (lax.psum_scatter(lines, axis, tiled=True).reshape(-1), 0, [])
    for b in pieces:
        part = b[0]
        finished.append(vector[at : at + part.size].reshape(part.shape))
        at += part.size
    return tuple(finished)


def copy_for_each(shard, axis):
    copies = jnp.broadcast_to(shard, (lax.axis_size(axis), *shard.shape))
    return lax.all_to_all(copies, axis, split_axis=0, concat_axis=0, tiled=True)


def over_copies(shard, axis):
    return copy_for_each(shard, axis).astype(jnp.float32).sum(axis=0)


def sent_together(arrays, axis, dim, along):
    both = jnp.concatenate(arrays, axis=along)
    filled, at, finished = (lax.all_gather(both, axis, axis=dim, tiled=True), 0, [])
    for a in arrays:
        finished.append(lax.slice_in_dim(filled, at, at + a.shape[along], axis=along))
        at += a.shape[along]
    return tuple(finished)


def normalize(values):
    return values * lax.rsqrt(jnp.mean(values * values, axis=-1, keepdims=True) + epsilon)


def attend(queries, key_rows, value_rows, head_count, key_mask):
    query_rows = queries.shape[0]
    key_total = key_rows.shape[0]
    channels = queries.shape[1]
    head_size = channels // head_count
    group = min(4, head_count)
    groups = head_count // group
    head_query = queries.reshape(query_rows, groups, group, head_size).transpose(1, 0, 2, 3)
    head_key = key_rows.reshape(key_total, groups, group, head_size).transpose(1, 0, 2, 3)
    head_value = value_rows.reshape(key_total, groups, group, head_size).transpose(1, 0, 2, 3)

    @jax.checkpoint
    def one_group(element):
        grouped_query_rows, grouped_key_rows, grouped_value_rows = element
        logit_table = (
            jnp.einsum(
                "ygq,pgq->gyp",
                grouped_query_rows,
                grouped_key_rows,
                preferred_element_type=jnp.float32,
            )
            * logit_scale
        )
        if key_mask is not None:
            logit_table = jnp.where(key_mask[None, None, :], logit_table, -1e30)
        logit_table = logit_table - lax.stop_gradient(jnp.max(logit_table, axis=-1, keepdims=True))
        exponent = jnp.exp(logit_table)
        attention_weight = (exponent / jnp.sum(exponent, axis=-1, keepdims=True)).astype(
            jnp.bfloat16
        )
        grouped_mixture = jnp.einsum(
            "yex,xyb->eyb", attention_weight, grouped_value_rows, preferred_element_type=jnp.float32
        )
        return grouped_mixture.astype(jnp.bfloat16)

    mixed_rows = lax.map(one_group, (head_query, head_key, head_value))
    return mixed_rows.transpose(1, 0, 2, 3).reshape(query_rows, channels)


def fine_attention(tokens, qkv_weight, patch_count):
    channels = tokens.shape[1]
    normed = normalize(tokens.astype(jnp.float32)).astype(jnp.bfloat16)
    packed = jnp.dot(normed, qkv_weight, preferred_element_type=jnp.float32).astype(jnp.bfloat16)
    slot_count = tokens.shape[0] // PATCH
    blocks = packed.reshape(slot_count, PATCH, 3 * channels)

    def one_patch(element):
        patch_rows, length = element
        key_mask = jnp.arange(PATCH) < length
        return attend(
            patch_rows[:, :channels],
            patch_rows[:, channels : 2 * channels],
            patch_rows[:, 2 * channels :],
            channels // HD,
            key_mask,
        )

    return lax.map(one_patch, (blocks, patch_count)).reshape(tokens.shape[0], channels)


def parent_table(offset):
    return (offset[:, None] == jnp.arange(Q_DEV + SPILL, dtype=jnp.int32)[None, :]).astype(
        jnp.float32
    )


def pool_counts(live_mask, offset):
    return jnp.dot(live_mask[None, :], parent_table(offset))[0]


def pool_forward(out_weight, pooling, tokens, mixed_rows, live_mask, offset):
    fine_out = (
        tokens.astype(jnp.float32)
        + jnp.dot(mixed_rows, out_weight.astype(jnp.bfloat16), preferred_element_type=jnp.float32)
    ).astype(jnp.bfloat16)
    projected = (
        jnp.dot(fine_out, pooling.astype(jnp.bfloat16), preferred_element_type=jnp.float32)
        * live_mask[:, None]
    )
    summed = jnp.dot(parent_table(offset).T, projected)
    return (summed[:Q_DEV], summed[Q_DEV:])


def coarse_forward(own_sum, arrived, qkv_weight, divisor):
    summed = own_sum + jnp.pad(arrived, ((0, Q_DEV - SPILL), (0, 0)))
    coarse_in = jax.nn.gelu(summed / divisor[:, None]).astype(jnp.bfloat16)
    normed = normalize(coarse_in.astype(jnp.float32)).astype(jnp.bfloat16)
    packed = jnp.dot(
        normed, qkv_weight.astype(jnp.bfloat16), preferred_element_type=jnp.float32
    ).astype(jnp.bfloat16)
    channels = coarse_in.shape[1]
    return (
        coarse_in,
        packed[:, :channels],
        packed[:, channels : 2 * channels],
        packed[:, 2 * channels :],
    )


def coarse_attention(coarse_in, queries, key_rows, value_rows, far_keys, far_values, out_weight):
    all_keys = jnp.concatenate([key_rows, far_keys], 0).astype(jnp.bfloat16)
    all_values = jnp.concatenate([value_rows, far_values], 0).astype(jnp.bfloat16)
    mixed_rows = attend(queries, all_keys, all_values, queries.shape[1] // HD, None)
    return (
        coarse_in.astype(jnp.float32)
        + jnp.dot(mixed_rows, out_weight.astype(jnp.bfloat16), preferred_element_type=jnp.float32)
    ).astype(jnp.bfloat16)


def local(
    fine_points,
    parent,
    patch_count,
    qkv_fine,
    out_fine,
    pool_weight,
    qkv_coarse,
    out_coarse,
    cotangent,
):
    position = lax.axis_index("rep") * lax.axis_size("pts") + lax.axis_index("pts")
    offset = parent - position * Q_DEV
    live_mask = (jnp.arange(PATCH)[None, :] < patch_count[:, None]).reshape(-1).astype(jnp.float32)
    live_total = pool_counts(live_mask, offset)
    mixed_rows = fine_attention(fine_points, qkv_fine, patch_count)

    def pool_part(out_weight, pooling):
        return pool_forward(out_weight, pooling, fine_points, mixed_rows, live_mask, offset)

    (own_sum, spill_sum), first_back = jax.vjp(
        pool_part, out_fine.astype(jnp.float32), pool_weight.astype(jnp.float32)
    )
    arrived, arrived_count = from_behind((spill_sum, live_total[Q_DEV:]), "pts", 1)
    divisor = jnp.maximum(live_total[:Q_DEV] + jnp.pad(arrived_count, (0, Q_DEV - SPILL)), 1.0)

    def coarse_part(own_part, arrived_part, qkv_part):
        return coarse_forward(own_part, arrived_part, qkv_part, divisor)

    (coarse_in, queries, key_rows, value_rows), second_back = jax.vjp(
        coarse_part, own_sum, arrived, qkv_coarse.astype(jnp.float32)
    )
    far_keys, far_values = swapped((key_rows, value_rows), "pts", 0)
    coarse_rows, third_back = jax.vjp(
        coarse_attention,
        coarse_in,
        queries,
        key_rows.astype(jnp.float32),
        value_rows.astype(jnp.float32),
        far_keys.astype(jnp.float32),
        far_values.astype(jnp.float32),
        out_coarse.astype(jnp.float32),
    )
    grad_in, grad_query, grad_key, grad_value, grad_far_key, grad_far_value, grad_out_coarse = (
        third_back(cotangent)
    )
    back_key, back_value = swapped(
        (grad_far_key.astype(jnp.bfloat16), grad_far_value.astype(jnp.bfloat16)), "pts", 0
    )
    total_key = (grad_key + back_key.astype(jnp.float32)).astype(jnp.bfloat16)
    total_value = (grad_value + back_value.astype(jnp.float32)).astype(jnp.bfloat16)
    grad_own, grad_arrived, grad_qkv_coarse = second_back(
        (grad_in, grad_query, total_key, total_value)
    )
    grad_spill = from_behind(grad_arrived, "pts", -1)
    grad_out_fine, grad_pool = first_back((grad_own, grad_spill))
    shares = sum_together(
        (grad_out_fine, grad_pool, grad_qkv_coarse, grad_out_coarse), "pts", (0, 0, 0, 0)
    )
    rounded = tuple((value.astype(jnp.bfloat16) for value in shares))
    share_sum = (
        over_copies(rounded[0], "rep").astype(jnp.float32),
        over_copies(rounded[1], "rep").astype(jnp.float32),
        over_copies(rounded[2], "rep").astype(jnp.float32),
        over_copies(rounded[3], "rep").astype(jnp.float32),
    )
    summed_shares = tuple((value.astype(jnp.bfloat16) for value in share_sum))
    finished = (
        *sent_together((summed_shares[0], summed_shares[1]), "pts", 0, 1),
        *sent_together((summed_shares[2], summed_shares[3]), "pts", 0, 1),
    )
    return (coarse_rows, finished[0], finished[1], finished[2], finished[3])


def solution(mesh):
    placed = (
        P(("rep", "pts"), None),
        P(("rep", "pts")),
        P(("rep", "pts")),
        P(),
        P(),
        P(),
        P(),
        P(),
        P(("rep", "pts"), None),
    )
    return jax.shard_map(
        local,
        mesh=mesh,
        in_specs=placed,
        out_specs=(P(("rep", "pts"), None), P(), P(), P(), P()),
        check_vma=False,
    )
```

profile of v0, /device:TPU:1, one launch (start us, length us, event | category | flops | bytes accessed | tf_op | source)
XLA Modules:
  0.0 494.7 jit_solution(16877470785943088793)
XLA Ops:
  9.2 6.3 %collective-permute-start.1 = (f32[32]{0:T(128)S(1)}, f32[32]{0:T(128)S(1)}, u32[]{:S(2)}, u32[]{:S(2)}) collective-permute-start(f32[32]{0:T(128)S(1)} %slice.81), channel_id=1, source_target_pairs={{0,1},{1,2},{2,3},{3,4},{4,5},{5,6},{6,7},{7,8},{8,9},{9,10},{10,1... | collective-permute-start | bytes 392 | tf_op jit(solution)/shard_map/ppermute | solution.py:19
  19.7 72.1 %while.48 = (s32[]{:T(128)}, bf16[4,1024,4,16]{1,3,2,0:T(8,128)(2,1)S(1)}, bf16[4,1024,4,16]{1,3,2,0:T(8,128)(2,1)}, bf16[4,1024,4,16]{1,3,2,0:T(8,128)(2,1)}, b...) while((s32[]{:T(128)}, bf16[4,1024,4,16]{1,3,2,0:T(8,128)(2,1)S(1)}, ...), condition=%wide.region_4.5_spmd.clone, body=%wide.region_1.4_spmd.clone.sunk | while | flops 293668864 | bytes 34115664 | solution.py:104
  20.5 10.3 %fusion.307 = (f32[4,1024]{1,0:T(4,128)S(1)}, f32[4,1024,1024]{1,2,0:T(8,128)}) fusion(pred[1024]{0:T(1024)(128)(4,1)S(1)} %iota_compare_fusion.9, bf16[4,1024,4,16]{1,3,2,0:T(8,128)(2,1)S(1)} %get-tuple-element.489, s32[]{:T(128)} %get-tuple-element.478, bf16[4,1024,4,16]{1,3,2,0:T(8,128)(2,1)} %get-tuple-element.488), kind=kOutput, calls=%fused_computation.186.clone.1 | convolution fusion | flops 150995968 | bytes 17057792 | tf_op jit(solution)/shard_map/while/body/eval_jaxpr/while/body/eval_jaxpr/checkpoint/sub | solution.py:94
  30.8 7.1 %fusion.308 = bf16[4,1024,4,16]{1,3,2,0:T(8,128)(2,1)S(1)} fusion(bf16[4,1024,4,16]{1,3,2,0:T(8,128)(2,1)S(1)} %get-tuple-element.479, s32[]{:T(128)} %get-tuple-element.478, f32[4,1024,1024]{1,2,0:T(8,128)} %get-tuple-element.469, f32[4,1024]{1,0:T(4,128)S(1)} %get-tuple-element.470, bf16[4,1024,4,16]{1,3,2,0:T(8,128)(2,1)} %get-tuple-element.487), kind=kOutput, calls=%fused_computation.78.clone.1 | convolution fusion | flops 142671872 | bytes 17056768 | tf_op jit(solution)/shard_map/while/body/eval_jaxpr/while/body/eval_jaxpr/checkpoint/yex,xyb->eyb/dot_general | solution.py:99
  38.5 10.3 %fusion.307 = (f32[4,1024]{1,0:T(4,128)S(1)}, f32[4,1024,1024]{1,2,0:T(8,128)}) fusion(pred[1024]{0:T(1024)(128)(4,1)S(1)} %iota_compare_fusion.9, bf16[4,1024,4,16]{1,3,2,0:T(8,128)(2,1)S(1)} %get-tuple-element.489, s32[]{:T(128)} %get-tuple-element.478, bf16[4,1024,4,16]{1,3,2,0:T(8,128)(2,1)} %get-tuple-element.488), kind=kOutput, calls=%fused_computation.186.clone.1 | convolution fusion | flops 150995968 | bytes 17057792 | tf_op jit(solution)/shard_map/while/body/eval_jaxpr/while/body/eval_jaxpr/checkpoint/sub | solution.py:94
  48.8 7.1 %fusion.308 = bf16[4,1024,4,16]{1,3,2,0:T(8,128)(2,1)S(1)} fusion(bf16[4,1024,4,16]{1,3,2,0:T(8,128)(2,1)S(1)} %get-tuple-element.479, s32[]{:T(128)} %get-tuple-element.478, f32[4,1024,1024]{1,2,0:T(8,128)} %get-tuple-element.469, f32[4,1024]{1,0:T(4,128)S(1)} %get-tuple-element.470, bf16[4,1024,4,16]{1,3,2,0:T(8,128)(2,1)} %get-tuple-element.487), kind=kOutput, calls=%fused_computation.78.clone.1 | convolution fusion | flops 142671872 | bytes 17056768 | tf_op jit(solution)/shard_map/while/body/eval_jaxpr/while/body/eval_jaxpr/checkpoint/yex,xyb->eyb/dot_general | solution.py:99
  56.5 10.3 %fusion.307 = (f32[4,1024]{1,0:T(4,128)S(1)}, f32[4,1024,1024]{1,2,0:T(8,128)}) fusion(pred[1024]{0:T(1024)(128)(4,1)S(1)} %iota_compare_fusion.9, bf16[4,1024,4,16]{1,3,2,0:T(8,128)(2,1)S(1)} %get-tuple-element.489, s32[]{:T(128)} %get-tuple-element.478, bf16[4,1024,4,16]{1,3,2,0:T(8,128)(2,1)} %get-tuple-element.488), kind=kOutput, calls=%fused_computation.186.clone.1 | convolution fusion | flops 150995968 | bytes 17057792 | tf_op jit(solution)/shard_map/while/body/eval_jaxpr/while/body/eval_jaxpr/checkpoint/sub | solution.py:94
  66.8 7.1 %fusion.308 = bf16[4,1024,4,16]{1,3,2,0:T(8,128)(2,1)S(1)} fusion(bf16[4,1024,4,16]{1,3,2,0:T(8,128)(2,1)S(1)} %get-tuple-element.479, s32[]{:T(128)} %get-tuple-element.478, f32[4,1024,1024]{1,2,0:T(8,128)} %get-tuple-element.469, f32[4,1024]{1,0:T(4,128)S(1)} %get-tuple-element.470, bf16[4,1024,4,16]{1,3,2,0:T(8,128)(2,1)} %get-tuple-element.487), kind=kOutput, calls=%fused_computation.78.clone.1 | convolution fusion | flops 142671872 | bytes 17056768 | tf_op jit(solution)/shard_map/while/body/eval_jaxpr/while/body/eval_jaxpr/checkpoint/yex,xyb->eyb/dot_general | solution.py:99
  74.5 10.3 %fusion.307 = (f32[4,1024]{1,0:T(4,128)S(1)}, f32[4,1024,1024]{1,2,0:T(8,128)}) fusion(pred[1024]{0:T(1024)(128)(4,1)S(1)} %iota_compare_fusion.9, bf16[4,1024,4,16]{1,3,2,0:T(8,128)(2,1)S(1)} %get-tuple-element.489, s32[]{:T(128)} %get-tuple-element.478, bf16[4,1024,4,16]{1,3,2,0:T(8,128)(2,1)} %get-tuple-element.488), kind=kOutput, calls=%fused_computation.186.clone.1 | convolution fusion | flops 150995968 | bytes 17057792 | tf_op jit(solution)/shard_map/while/body/eval_jaxpr/while/body/eval_jaxpr/checkpoint/sub | solution.py:94
  84.8 7.1 %fusion.308 = bf16[4,1024,4,16]{1,3,2,0:T(8,128)(2,1)S(1)} fusion(bf16[4,1024,4,16]{1,3,2,0:T(8,128)(2,1)S(1)} %get-tuple-element.479, s32[]{:T(128)} %get-tuple-element.478, f32[4,1024,1024]{1,2,0:T(8,128)} %get-tuple-element.469, f32[4,1024]{1,0:T(4,128)S(1)} %get-tuple-element.470, bf16[4,1024,4,16]{1,3,2,0:T(8,128)(2,1)} %get-tuple-element.487), kind=kOutput, calls=%fused_computation.78.clone.1 | convolution fusion | flops 142671872 | bytes 17056768 | tf_op jit(solution)/shard_map/while/body/eval_jaxpr/while/body/eval_jaxpr/checkpoint/yex,xyb->eyb/dot_general | solution.py:99
  109.2 106.5 %while.47 = (s32[]{:T(128)}, bf16[8,256,4,16]{1,3,2,0:T(8,128)(2,1)}, bf16[8,512,4,16]{1,3,2,0:T(8,128)(2,1)}, bf16[8,512,4,16]{1,3,2,0:T(8,128)(2,1)}, bf16[8,2...) while((s32[]{:T(128)}, ...), condition=%wide.region_14.15_spmd, body=%wide.region_10.14_spmd.sunk | while | flops 147938304 | bytes 8568965 | solution.py:104
  113.1 2.2 fusion.300
  115.2 2.9 fusion.302
  118.1 2.9 fusion.301
  128.5 2.9 fusion.302
  131.4 2.9 fusion.301
  141.9 2.9 fusion.302
  144.7 2.9 fusion.301
  155.2 2.9 fusion.302
  158.0 2.9 fusion.301
  168.5 2.9 fusion.302
  171.3 2.9 fusion.301
  179.6 2.2 fusion.300
  181.8 2.9 fusion.302
  184.6 2.9 fusion.301
  195.1 2.9 fusion.302
  197.9 2.9 fusion.301
  208.4 2.9 fusion.302
  211.2 2.9 fusion.301
  219.7 28.9 %while.46 = (s32[]{:T(128)}, bf16[8,256,4,16]{1,3,2,0:T(8,128)(2,1)S(1)}, bf16[8,512,4,16]{1,3,2,0:T(8,128)(2,1)}, bf16[8,256,4,16]{1,3,2,0:T(8,128)(2,1)}, bf16[8,512,4,16]{1,3,2,0:T(8,128)(2,1)}, /*index=5*/s32[]{:T(128)}) while((s32[]{:T(128)}, bf16[8,256,4,16]{1,3,2,0:T(8,128)(2,1)S(1)}, bf16[8,512,4,16]{1,3,2,0:T(8,128)(2,1)}, ...), condition=%wide.region_9.10_spmd, body=%wide.region_6.9_spmd.sunk | while | flops 54020096 | bytes 306245 | solution.py:104
  255.2 2.4 collective-permute-start.6
  261.3 2.7 collective-permute-done.6
  264.1 3.1 fusion.135
  267.2 3.2 fusion.149
  270.4 3.0 fusion.146
  276.2 3.7 maximum_convert_fusion
  279.9 5.4 %reshape.164 = f32[9728,128]{1,0:T(8,128)} reshape(f32[32,38912]{1,0:T(8,128)} %maximum_convert_fusion) | data formatting | bytes 9961472 | tf_op jit(solution)/shard_map/reshape | solution.py:38
  285.3 104.7 %reduce-scatter.2.cloned.1.call-done = f32[304,128]{1,0:T(8,128)} async-done(((f32[9728,128]{1,0:T(8,128)}), f32[304,128]{1,0:T(8,128)}) %reduce-scatter.2.cloned.1.call-update) | async-done | bytes 155664 | tf_op jit(solution)/shard_map/reduce_scatter | solution.py:39
  391.6 4.1 all-to-all-start.3
  395.7 5.3 %all-to-all-done.3 = bf16[8,16,512]{2,1,0:T(8,128)(2,1)S(1)} async-done(((bf16[8,16,512]{2,1,0:T(8,128)(2,1)}), bf16[8,16,512]{2,1,0:T(8,128)(2,1)S(1)}, u32[]{:S(2)}, u32[]{:S(2)}) %all-to-all-start.3) | async-done | bytes 131104 | tf_op jit(solution)/shard_map/all_to_all | solution.py:49
  401.8 3.5 all-to-all-start.2
  405.4 6.5 %all-to-all-done.2 = bf16[8,16,1536]{2,1,0:T(8,128)(2,1)S(1)} async-done(((bf16[8,16,1536]{2,1,0:T(8,128)(2,1)}), bf16[8,16,1536]{2,1,0:T(8,128)(2,1)S(1)}, u32[]{:S(2)}, u32[]{:S(2)}) %all-to-all-start.2) | async-done | bytes 393248 | tf_op jit(solution)/shard_map/all_to_all | solution.py:49
  413.2 3.3 all-to-all-start
  416.6 5.0 %all-to-all-done = bf16[8,8,256]{2,1,0:T(8,128)(2,1)S(1)} async-done(((bf16[8,8,256]{2,1,0:T(8,128)(2,1)}), bf16[8,8,256]{2,1,0:T(8,128)(2,1)S(1)}, u32[]{:S(2)}, u32[]{:S(2)}) %all-to-all-start) | async-done | bytes 32800 | tf_op jit(solution)/shard_map/all_to_all | solution.py:49
  422.2 3.4 all-to-all-start.1
  426.7 4.1 all-to-all-done.1
  430.8 51.1 %all_gather.6 = bf16[256,768]{1,0:T(8,128)(2,1)S(1)} all-gather(bf16[8,768]{1,0:T(8,128)(2,1)S(1)} %pad_maximum_fusion.1), channel_id=1, replica_groups=mesh['rep'=8,'pts'=32] {'pts'}, dimensions={0}, use_global_device_ids=true | all-gather | bytes 405504 | tf_op jit(solution)/shard_map/all_gather | solution.py:58
  483.4 2.7 slice.107
  (192 shorter events, 136.1 us)
Async XLA Ops:
  7.2 91.0 %copy-start = (bf16[512,1536]{1,0:T(8,128)(2,1)S(1)}, bf16[512,1536]{1,0:T(8,128)(2,1)}, u32[]{:S(2)}) copy-start(bf16[512,1536]{1,0:T(8,128)(2,1)} %param.21) | copy-start | bytes 4718596
  7.2 382.8 %reduce-scatter.2.cloned.1.call-start = ((), (), s32[]{:S(2)}) async-start(), calls=%async_computation.5 | async-start | bytes 5136384 | tf_op jit(solution)/shard_map/reduce_scatter | solution.py:39
  9.2 87.1 %collective-permute-start.1 = (f32[32]{0:T(128)S(1)}, f32[32]{0:T(128)S(1)}, u32[]{:S(2)}, u32[]{:S(2)}) collective-permute-start(f32[32]{0:T(128)S(1)} %slice.81), channel_id=1, source_target_pairs={{0,1},{1,2},{2,3},{3,4},{4,5},{5,6},{6,7},{7,8},{8,9},{9,10},{10,1... | collective-permute-start | bytes 392 | tf_op jit(solution)/shard_map/ppermute | solution.py:19
  19.7 72.2 %copy-start.1 = (bf16[1024,256]{1,0:T(8,128)(2,1)S(1)}, bf16[1024,256]{1,0:T(8,128)(2,1)}, u32[]{:S(2)}) copy-start(bf16[1024,256]{1,0:T(8,128)(2,1)} %param.15) | copy-start | bytes 1572868
  19.7 73.6 %copy-start.13 = (bf16[256,512]{1,0:T(8,128)(2,1)S(1)}, bf16[256,512]{1,0:T(8,128)(2,1)}, u32[]{:S(2)}) copy-start(bf16[256,512]{1,0:T(8,128)(2,1)} %param.20) | copy-start | bytes 786436
  91.9 2.4 copy-start.11
  93.4 4.6 copy-start.10
  94.3 5.4 %copy-start.6 = (f32[288,512]{1,0:T(8,128)}, f32[288,512]{1,0:T(8,128)S(1)}, u32[]{:S(2)}) copy-start(f32[288,512]{1,0:T(8,128)S(1)} %fusion.127) | copy-start | bytes 1769476
  94.3 3.2 collective-permute-start
  97.6 0.6 copy-start.15
  98.2 2.0 copy-start.5
  98.2 2.0 copy-start.8
  99.7 3.0 copy-start.12
  99.7 3.8 collective-permute-start.2
  99.7 4.8 collective-permute-start.3
  217.4 32.5 %collective-permute-start.4 = (bf16[256,512]{0,1:T(8,128)(2,1)}, bf16[256,512]{0,1:T(8,128)(2,1)}, u32[]{:S(2)}, u32[]{:S(2)}) collective-permute-start(bf16[256,512]{0,1:T(8,128)(2,1)} %bitcast.41), channel_id=1, source_target_pairs={{0,1},{1,0},{2,3},{3,2},{4,5},{5,4},{6,7},{7,6},{8,9},{9,8},{10,11... | collective-permute-start | bytes 786440 | tf_op jit(solution)/shard_map/ppermute | solution.py:25
  219.5 31.5 %collective-permute-start.5 = (bf16[256,512]{0,1:T(8,128)(2,1)}, bf16[256,512]{0,1:T(8,128)(2,1)}, u32[]{:S(2)}, u32[]{:S(2)}) collective-permute-start(bf16[256,512]{0,1:T(8,128)(2,1)} %bitcast.44), channel_id=1, source_target_pairs={{0,1},{1,0},{2,3},{3,2},{4,5},{5,4},{6,7},{7,6},{8,9},{9,8},{10,11... | collective-permute-start | bytes 786440 | tf_op jit(solution)/shard_map/ppermute | solution.py:25
  248.6 5.2 %copy-start.3 = (bf16[8,256,4,16]{1,3,2,0:T(8,128)(2,1)}, bf16[8,256,4,16]{1,3,2,0:T(8,128)(2,1)S(1)}, u32[]{:S(2)}) copy-start(bf16[8,256,4,16]{1,3,2,0:T(8,128)(2,1)S(1)} %get-tuple-element.243) | copy-start | bytes 786436
  252.0 1.8 copy-start.7
  252.0 1.8 copy-start.16
  253.8 3.8 copy-start.14
  254.4 0.8 copy-start.2
  255.2 8.9 %collective-permute-start.6 = (f32[32,512]{1,0:T(8,128)S(1)}, f32[32,512]{1,0:T(8,128)S(1)}, u32[]{:S(2)}, u32[]{:S(2)}) collective-permute-start(f32[32,512]{1,0:T(8,128)S(1)} %pad.48), channel_id=1, source_target_pairs={{1,0},{2,1},{3,2},{4,3},{5,4},{6,5},{7,6},{8,7},{9,8},{10,9},{11,1... | collective-permute-start | bytes 196616 | tf_op jit(solution)/shard_map/ppermute | solution.py:19
  285.3 140.3 %copy-start.4 = (bf16[8,256,4,16]{1,3,2,0:T(8,128)(2,1)S(1)}, bf16[8,256,4,16]{1,3,2,0:T(8,128)(2,1)}, u32[]{:S(2)}) copy-start(bf16[8,256,4,16]{1,3,2,0:T(8,128)(2,1)} %copy-done.3) | copy-start | bytes 786436
  285.3 140.3 %copy-start.9 = (bf16[512,512]{1,0:T(8,128)(2,1)S(1)}, bf16[512,512]{1,0:T(8,128)(2,1)}, u32[]{:S(2)}) copy-start(bf16[512,512]{1,0:T(8,128)(2,1)} %param.22) | copy-start | bytes 1572868
  391.6 9.5 %all-to-all-start.3 = ((bf16[8,16,512]{2,1,0:T(8,128)(2,1)}), bf16[8,16,512]{2,1,0:T(8,128)(2,1)S(1)}, u32[]{:S(2)}, u32[]{:S(2)}) async-start(bf16[8,16,512]{2,1,0:T(8,128)(2,1)} %broadcast_in_dim.98), calls=%async_computation.4 | async-start | bytes 262144 | tf_op jit(solution)/shard_map/all_to_all | solution.py:49
  401.8 10.0 %all-to-all-start.2 = ((bf16[8,16,1536]{2,1,0:T(8,128)(2,1)}), bf16[8,16,1536]{2,1,0:T(8,128)(2,1)S(1)}, u32[]{:S(2)}, u32[]{:S(2)}) async-start(bf16[8,16,1536]{2,1,0:T(8,128)(2,1)} %broadcast_in_dim.97), calls=%async_computation.3 | async-start | bytes 786432 | tf_op jit(solution)/shard_map/all_to_all | solution.py:49
  405.3 78.1 %all-gather.2.cloned.1.call-start = ((), (), s32[]{:S(2)}) async-start(), calls=%async_computation.6 | async-start | bytes 2162688 | tf_op jit(solution)/shard_map/all_gather | solution.py:58
  413.2 8.4 %all-to-all-start = ((bf16[8,8,256]{2,1,0:T(8,128)(2,1)}), bf16[8,8,256]{2,1,0:T(8,128)(2,1)S(1)}, u32[]{:S(2)}, u32[]{:S(2)}) async-start(bf16[8,8,256]{2,1,0:T(8,128)(2,1)} %broadcast_in_dim.95), calls=%async_computation.1 | async-start | bytes 65536 | tf_op jit(solution)/shard_map/all_to_all | solution.py:49
  422.2 8.6 %all-to-all-start.1 = ((bf16[8,8,512]{2,1,0:T(8,128)(2,1)}), bf16[8,8,512]{2,1,0:T(8,128)(2,1)S(1)}, u32[]{:S(2)}, u32[]{:S(2)}) async-start(bf16[8,8,512]{2,1,0:T(8,128)(2,1)} %broadcast_in_dim.96), calls=%async_computation.2 | async-start | bytes 131072 | tf_op jit(solution)/shard_map/all_to_all | solution.py:49
Sparse Core Ops, SparseCore 0:
  285.4 104.5 reduce-scatter.1
  412.7 55.6 all-gather.1
where the time goes:
time: 498 us; the launch traced here: 495 us
  matrix products  211 us (42%)
  waiting for transfers between devices  130 us (26%)
  blocking collectives  51.1 us (10%)
  local copies, waits for them, and re-layouts  47.2 us (9%)
  starting transfers between devices  25.9 us (5%)
  between operations  15.3 us (3%)
  other arithmetic  14.2 us (3%)
    reduce_scatter x1, waiting for transfers between devices, sum_together(): lax.psum_scatter(lines, axis, tiled=True).reshape(-1)  105 us
    dot_general x28, matrix products, one_group(): jnp.einsum('yex,xyb->eyb', attention_weight, grouped_value_rows, preferre...  72.8 us
    sub x20, matrix products, one_group(): logit_table - lax.stop_gradient(jnp.max(logit_table, axis=-1, keepdims=Tr...  72.5 us
    all_gather x1, blocking collectives, sent_together(): lax.all_gather(both, axis, axis=dim, tiled=True)  51.1 us
    dot_general x16, matrix products, one_group(): jnp.einsum('ygq,pgq->gyp', grouped_query_rows, grouped_key_rows, preferre...  46 us
    all_to_all x4, waiting for transfers between devices, copy_for_each(): return lax.all_to_all(copies, axis, split_axis=0, concat_axis=0, tiled=True)  20.9 us
    all_to_all x4, starting transfers between devices, copy_for_each(): return lax.all_to_all(copies, axis, split_axis=0, concat_axis=0, tiled=True)  14.2 us
    squeeze x16, local copies, waits for them, and re-layouts, attend(): mixed_rows = lax.map(one_group, (head_query, head_key, head_value))  13.3 us
  transfers between devices with their start and end apart: 13, of which 7 were waited for; matrix products, arithmetic and copies ran while one was open for 25% of the time, Pallas kernels for 0%

commit v1 on v0

v1 whole, which is shorter than its diff:
```python
import jax
import jax.numpy as jnp
from jax import lax
from jax.experimental import pallas as pl
from jax.experimental.pallas import tpu as pltpu
from jax.sharding import PartitionSpec as P

F32 = jnp.float32
BF = jnp.bfloat16
EPS = 1e-6
LOG2E = 1.4426950408889634
LN2 = 0.6931471805599453
SAFE = 80.0
MESH = pl.DeviceIdType.MESH
VM = pl.BlockSpec(memory_space=pltpu.VMEM)
SM = pl.BlockSpec(memory_space=pltpu.SMEM)

NN = (((1,), (0,)), ((), ()))
NT = (((1,), (1,)), ((), ()))
TN = (((0,), (0,)), ((), ()))
TT = (((0,), (1,)), ((), ()))


def mm(a, b, dims=NN):
    return lax.dot_general(a, b, dims, preferred_element_type=F32)


def normalize(values):
    return values * lax.rsqrt(jnp.mean(values * values, axis=-1, keepdims=True) + EPS)


def split_dot(a, b):
    high = a.astype(BF)
    low = (a - high.astype(F32)).astype(BF)
    return mm(high, b) + mm(low, b)


def head_rows(rows, width):
    return lax.broadcasted_iota(jnp.int32, (rows, width), 0) // 16


def score_bound(qt, k):
    channels = qt.shape[0]
    heads = (
        lax.broadcasted_iota(jnp.int32, (channels, 128), 0) // 16
        == lax.broadcasted_iota(jnp.int32, (channels, 128), 1)
    ).astype(BF)
    kf = k.astype(F32)
    k2 = mm((kf * kf).astype(BF), heads)
    q = qt.astype(F32)
    q2 = (q * q).reshape(channels // 16, 16, qt.shape[1]).sum(axis=1)
    return jnp.max(q2) * jnp.max(k2)


def fine_kernel(cnt_ref, off_ref, x_ref, w_ref, ow_ref, ab_ref, k_ref, qt_ref, va_ref, mt_ref):
    count = cnt_ref[0]
    x = x_ref[...]
    n = normalize(x.astype(F32)).astype(BF)
    k_ref[...] = mm(n, w_ref[:, 256:512]).astype(BF)
    qt_ref[...] = (mm(w_ref[:, :256], n, TT) * (0.25 * LOG2E)).astype(BF)
    vt = mm(w_ref[:, 512:], n, TT).astype(BF)
    live = lax.broadcasted_iota(jnp.int32, (1, 1024), 1) < count
    ones = jnp.where(jnp.broadcast_to(live, (16, 1024)), 1.0, 0.0).astype(BF)
    for h in range(16):
        rows = vt[h * 16 : h * 16 + 16, :].astype(F32)
        va_ref[h, 0:16, :] = jnp.where(live, rows, 0.0).astype(BF)
        va_ref[h, 16:32, :] = ones
    bound = score_bound(qt_ref[...], k_ref[...])
    quick = bound < SAFE * SAFE

    def attend(shift):
        def head(h, carry):
            half = pl.multiple_of((h // 8) * 128, 128)
            keys = k_ref[:, pl.ds(half, 128)]
            chosen = head_rows(128, 256) == h % 8
            row = pl.multiple_of(h * 16, 16)
            for t in range(4):
                cols = slice(t * 256, t * 256 + 256)
                part = qt_ref[pl.ds(half, 128), cols]
                qm = jnp.where(chosen, part, jnp.zeros_like(part))
                s = mm(keys, qm)
                if shift:
                    alive = lax.broadcasted_iota(jnp.int32, (1024, 256), 0) < count
                    s = jnp.where(alive, s, -1e30)
                    s = s - jnp.max(s, axis=0, keepdims=True)
                p = jnp.exp2(s).astype(BF)
                o = mm(va_ref[h], p)
                mt_ref[pl.ds(row, 16), cols] = (o[:16] / o[16:]).astype(BF)
            return carry

        lax.fori_loop(0, 16, head, 0)

    @pl.when(quick)
    def _():
        attend(False)

    @pl.when(jnp.logical_not(quick))
    def _():
        attend(True)

    table = jnp.where(
        (lax.broadcasted_iota(jnp.int32, (288, 1024), 0) == off_ref[...]) & live, 1.0, 0.0
    )
    total = jnp.sum(table, axis=1, keepdims=True)
    table = table.astype(BF)
    b = mm(table, mt_ref[...], NT)
    ab_ref[:, :256] = mm(table, x) + split_dot(b, ow_ref[...])
    ab_ref[:, 256:512] = b
    ab_ref[:, 512:] = jnp.broadcast_to(total, (288, 128))


def fine_call(count, offset, x, w, ow):
    return pl.pallas_call(
        fine_kernel,
        out_shape=jax.ShapeDtypeStruct((288, 640), F32),
        in_specs=[SM, VM, VM, VM, VM],
        out_specs=VM,
        scratch_shapes=[
            pltpu.VMEM((1024, 256), BF),
            pltpu.VMEM((256, 1024), BF),
            pltpu.VMEM((16, 32, 1024), BF),
            pltpu.VMEM((256, 1024), BF),
        ],
        compiler_params=pltpu.CompilerParams(vmem_limit_bytes=56 * 1024 * 1024),
        name="fine",
    )(count, offset, x, w, ow)


def pooled(ab_ref, arr_ref, first, last):
    top = ab_ref[:32, first:last] + arr_ref[:, first:last]
    return jnp.concatenate([top, ab_ref[32:256, first:last]], axis=0)


def pooled_mean(ab_ref, arr_ref, pw_ref):
    a = pooled(ab_ref, arr_ref, 0, 256)
    count = jnp.maximum(pooled(ab_ref, arr_ref, 512, 640)[:, :1], 1.0)
    return split_dot(a, pw_ref[...]) / count, count


GA = 0.7978845608028654
GB = 0.044715


def coarse_in_kernel(ab_ref, arr_ref, pw_ref, c_ref):
    u, _ = pooled_mean(ab_ref, arr_ref, pw_ref)
    c_ref[...] = (0.5 * u * (1.0 + jnp.tanh(GA * (u + GB * u * u * u)))).astype(BF)


def coarse_kernel(
    core_ref, c_ref, cf_ref, ct_ref, ctf_ref, w_ref, ow_ref,
    dn_ref, mix_ref, g_ref,
    n_ref, cot_ref, k_ref, v_ref, kt_ref, qt_ref, va_ref, dot_ref, ot_ref, dp_ref,
):
    core = core_ref[0]
    lo = pl.multiple_of(core * 256, 256)
    n_ref[:256] = normalize(c_ref[...].astype(F32)).astype(BF)
    n_ref[256:] = normalize(cf_ref[...].astype(F32)).astype(BF)
    cot_ref[:256] = ct_ref[...]
    cot_ref[256:] = ctf_ref[...]
    n = n_ref[...]
    wq = w_ref[:, pl.ds(lo, 256)]
    wk = w_ref[:, pl.ds(512 + lo, 256)]
    wv = w_ref[:, pl.ds(1024 + lo, 256)]
    qt_ref[...] = (mm(wq, n, TT) * (0.25 * LOG2E)).astype(BF)
    k_ref[...] = mm(n, wk).astype(BF)
    v_ref[...] = mm(n, wv).astype(BF)
    kt_ref[...] = mm(wk, n, TT).astype(BF)
    vt = mm(wv, n, TT).astype(BF)
    for h in range(16):
        va_ref[h, :16, :] = vt[h * 16 : h * 16 + 16, :]
        va_ref[h, 16:, :] = jnp.ones((16, 512), BF)
    dot_ref[...] = mm(ow_ref[pl.ds(lo, 256), :], cot_ref[...], NT)
    quick = score_bound(qt_ref[...], k_ref[...]) < SAFE * SAFE

    def attend(shift):
        def head(h, carry):
            half = pl.multiple_of((h // 8) * 128, 128)
            chosen = head_rows(128, 512) == h % 8
            row = pl.multiple_of(h * 16, 16)
            part = qt_ref[pl.ds(half, 128), :]
            qm = jnp.where(chosen, part, jnp.zeros_like(part))
            s = mm(k_ref[:, pl.ds(half, 128)], qm)
            if shift:
                s = s - jnp.max(s, axis=0, keepdims=True)
            p = jnp.exp2(s)
            pb = p.astype(BF)
            o = mm(va_ref[h], pb)
            inverse = 1.0 / o[16:]
            on = o[:16] * inverse
            ot_ref[pl.ds(row, 16), :] = on.astype(BF)
            do = dot_ref[pl.ds(row, 16), :] * inverse
            dob = do.astype(BF)
            delta = jnp.sum(dob.astype(F32) * on, axis=0, keepdims=True)
            tiled = jnp.concatenate([dob] * 8, axis=0)
            dom = jnp.where(chosen, tiled, jnp.zeros_like(tiled))
            dpt = mm(v_ref[:, pl.ds(half, 128)], dom)
            ds = (p * (dpt - delta)).astype(BF)
            dp_ref[pl.ds(row, 16), :] = (mm(kt_ref[pl.ds(row, 16), :], ds) * 0.25).astype(BF)
            dk = mm(qt_ref[pl.ds(row, 16), :], ds, NT) * LN2
            dp_ref[pl.ds(256 + row, 16), :] = dk.astype(BF)
            dp_ref[pl.ds(512 + row, 16), :] = mm(dob, pb, NT).astype(BF)
            return carry

        lax.fori_loop(0, 16, head, 0)

    @pl.when(quick)
    def _():
        attend(False)

    @pl.when(jnp.logical_not(quick))
    def _():
        attend(True)

    mix_ref[...] = jnp.transpose(ot_ref[...])
    dnt = (
        mm(wq, dp_ref[:256, :]) + mm(wk, dp_ref[256:512, :]) + mm(wv, dp_ref[512:, :])
    ).astype(BF)
    dn_ref[...] = jnp.transpose(dnt)
    nt = jnp.transpose(n_ref[...])
    for j in range(6):
        block = mm(nt, dp_ref[j * 128 : j * 128 + 128, :], NT).astype(BF)
        g_ref[j * 32 : j * 32 + 32] = block.reshape(32, 16, 128)
    for j in range(4):
        block = mm(ot_ref[...], cot_ref[:, j * 128 : j * 128 + 128]).astype(BF)
        g_ref[192 + j * 16 : 208 + j * 16] = block.reshape(16, 16, 128)


def coarse_call(core, c, cf, ct, ctf, w, ow):
    return pl.pallas_call(
        coarse_kernel,
        out_shape=(
            jax.ShapeDtypeStruct((512, 512), BF),
            jax.ShapeDtypeStruct((512, 256), BF),
            jax.ShapeDtypeStruct((256, 16, 128), BF),
        ),
        in_specs=[SM, VM, VM, VM, VM, VM, VM],
        out_specs=(VM, VM, VM),
        scratch_shapes=[
            pltpu.VMEM((512, 512), BF),
            pltpu.VMEM((512, 512), BF),
            pltpu.VMEM((512, 256), BF),
            pltpu.VMEM((512, 256), BF),
            pltpu.VMEM((256, 512), BF),
            pltpu.VMEM((256, 512), BF),
            pltpu.VMEM((16, 32, 512), BF),
            pltpu.VMEM((256, 512), F32),
            pltpu.VMEM((256, 512), BF),
            pltpu.VMEM((768, 512), BF),
        ],
        compiler_params=pltpu.CompilerParams(vmem_limit_bytes=56 * 1024 * 1024),
        name="coarse",
    )(core, c, cf, ct, ctf, w, ow)


def finish_kernel(
    core_ref, ab_ref, arr_ref, pw_ref, c_ref, ct_ref, dn_ref, dnf_ref, mix_ref, mixf_ref,
    ow_ref, out_ref, g_ref,
):
    core = core_ref[0]
    lo = pl.multiple_of(core * 256, 256)
    hi = pl.multiple_of(256 - core * 256, 256)
    c = c_ref[...].astype(F32)
    mixed = mm(mix_ref[:256], ow_ref[pl.ds(lo, 256), :]) + mm(mixf_ref[...], ow_ref[pl.ds(hi, 256), :])
    out_ref[...] = (c + mixed).astype(BF)
    dn = dn_ref[:256].astype(F32) + dnf_ref[...].astype(F32)
    r = lax.rsqrt(jnp.mean(c * c, axis=-1, keepdims=True) + EPS)
    inner = jnp.mean(dn * c, axis=-1, keepdims=True)
    dc = r * dn - c * (r * r * r * inner) + ct_ref[...].astype(F32)
    u, count = pooled_mean(ab_ref, arr_ref, pw_ref)
    th = jnp.tanh(GA * (u + GB * u * u * u))
    slope = 0.5 * (1.0 + th) + 0.5 * u * (1.0 - th * th) * (GA * (1.0 + 3.0 * GB * u * u))
    gs = (slope * dc / count).astype(BF)
    at = jnp.transpose(pooled(ab_ref, arr_ref, 0, 256)).astype(BF)
    bt = jnp.transpose(pooled(ab_ref, arr_ref, 256, 512)).astype(BF)
    gw = mm(gs, pw_ref[...], NT).astype(BF)
    for half in range(2):
        rows = slice(half * 128, half * 128 + 128)
        for j in range(4):
            block = mm(at[rows], gs[:, j * 128 : j * 128 + 128]).astype(BF)
            g_ref[half, j * 8 : j * 8 + 8] = block.reshape(8, 16, 128)
        for j in range(2):
            block = mm(bt[rows], gw[:, j * 128 : j * 128 + 128]).astype(BF)
            g_ref[half, 32 + j * 8 : 40 + j * 8] = block.reshape(8, 16, 128)


def reduce_kernel(
    big_ref, small_ref, gof_ref, gp_ref, gq_ref, goc_ref,
    g, full, sm, ra, rb, ha, hb, ra2, rb2, z, rz, zf, fa, fb, send, recv,
):
    rep = lax.axis_index("rep")
    pts = lax.axis_index("pts")
    x = rep % 4
    zlo = rep // 4
    y = pts // 8
    zhi = (pts // 2) % 4
    core = pts % 2
    zi = zhi * 2 + zlo

    def xpeer(d):
        return (zlo * 4 + (x + d) % 4, pts)

    def ypeer(d):
        return (rep, ((y + d) % 4) * 8 + zhi * 2 + core)

    def zpeer(d):
        other = (zi + d) % 8
        return ((other % 2) * 4 + x, y * 8 + (other // 2) * 2 + core)

    partner = (rep, pts + 1 - 2 * core)
    barrier = pltpu.get_barrier_semaphore()
    peers = [partner]
    peers += [xpeer(d) for d in (1, 2, 3)] + [ypeer(d) for d in (1, 2, 3)]
    peers += [zpeer(d) for d in range(1, 8)]
    for peer in peers:
        pl.semaphore_signal(barrier, inc=1, device_id=peer, device_id_type=MESH)
    pl.semaphore_wait(barrier, len(peers))

    counter = [0]

    def push(src, dst, peer):
        i = counter[0]
        counter[0] += 1
        copy = pltpu.make_async_remote_copy(
            src_ref=src, dst_ref=dst, send_sem=send.at[i], recv_sem=recv.at[i],
            device_id=peer, device_id_type=MESH,
        )
        copy.start()
        return copy

    swap = push(small_ref.at[1 - core], sm, partner)
    g[:256] = big_ref[...]
    g[304:] = jnp.zeros((16, 16, 128), BF)
    first = []
    for d in (1, 2, 3):
        to = (x + d) % 4
        first.append(push(g.at[pl.ds(to * 40, 40)], ra.at[d - 1], xpeer(d)))
    swap.wait()
    g[256:304] = (small_ref[core].astype(F32) + sm[...].astype(F32)).astype(BF)
    for d in (1, 2, 3):
        to = (y + d) % 4
        first.append(push(g.at[pl.ds(160 + to * 40, 40)], rb.at[d - 1], ypeer(d)))
    for copy in first:
        copy.wait()

    def add(own, slots, n):
        total = own.astype(F32)
        for d in range(n):
            total = total + slots[d].astype(F32)
        return total.astype(BF)

    ha[...] = add(g[pl.ds(x * 40, 40)], ra, 3)
    hb[...] = add(g[pl.ds(160 + y * 40, 40)], rb, 3)
    second = []
    for d in (1, 2, 3):
        second.append(push(ha.at[pl.ds(((y + d) % 4) * 10, 10)], ra2.at[d - 1], ypeer(d)))
        second.append(push(hb.at[pl.ds(((x + d) % 4) * 10, 10)], rb2.at[d - 1], xpeer(d)))
    for copy in second:
        copy.wait()
    z[:10] = add(ha[pl.ds(y * 10, 10)], ra2, 3)
    z[10:20] = add(hb[pl.ds(x * 10, 10)], rb2, 3)
    z[20:] = jnp.zeros((4, 16, 128), BF)
    third = []
    for d in range(1, 8):
        third.append(push(z.at[pl.ds(((zi + d) % 8) * 3, 3)], rz.at[d - 1], zpeer(d)))
    for copy in third:
        copy.wait()
    mine = pl.ds(zi * 3, 3)
    zf[mine] = add(z[mine], rz, 7)
    back = [push(zf.at[mine], zf.at[mine], zpeer(d)) for d in range(1, 8)]
    for copy in back:
        copy.wait()
    at, bt = pl.ds(y * 10, 10), pl.ds(x * 10, 10)
    fa[at] = zf[:10]
    fb[bt] = zf[10:20]
    back = []
    for d in (1, 2, 3):
        back.append(push(fa.at[at], fa.at[at], ypeer(d)))
        back.append(push(fb.at[bt], fb.at[bt], xpeer(d)))
    for copy in back:
        copy.wait()
    at, bt = pl.ds(x * 40, 40), pl.ds(160 + y * 40, 40)
    full[core, at] = fa[...]
    full[core, bt] = fb[...]
    back = []
    for d in (1, 2, 3):
        back.append(push(full.at[core, at], full.at[core, at], xpeer(d)))
        back.append(push(full.at[core, bt], full.at[core, bt], ypeer(d)))
    for copy in back:
        copy.wait()
    push(full.at[core], full.at[core], partner).wait()
    for c in range(2):
        for j in range(6):
            column = (j // 2) * 512 + c * 256 + (j % 2) * 128
            gq_ref[:, column : column + 128] = full[c, j * 32 : j * 32 + 32].reshape(512, 128)
        for j in range(4):
            rows = slice(c * 256, c * 256 + 256)
            tile = full[c, 192 + j * 16 : 208 + j * 16].reshape(256, 128)
            goc_ref[rows, j * 128 : j * 128 + 128] = tile
        rows = slice(c * 128, c * 128 + 128)
        for j in range(4):
            tile = full[c, 256 + j * 8 : 264 + j * 8].reshape(128, 128)
            gp_ref[rows, j * 128 : j * 128 + 128] = tile
        for j in range(2):
            tile = full[c, 288 + j * 8 : 296 + j * 8].reshape(128, 128)
            gof_ref[rows, j * 128 : j * 128 + 128] = tile


def reduce_call(big, small):
    def tiles(*n):
        return pltpu.VMEM((*n, 16, 128), BF)

    return pl.pallas_call(
        reduce_kernel,
        out_shape=(
            jax.ShapeDtypeStruct((256, 256), BF),
            jax.ShapeDtypeStruct((256, 512), BF),
            jax.ShapeDtypeStruct((512, 1536), BF),
            jax.ShapeDtypeStruct((512, 512), BF),
        ),
        in_specs=[VM, VM],
        out_specs=(VM, VM, VM, VM),
        scratch_shapes=[
            tiles(320), tiles(2, 320), tiles(48), tiles(3, 40), tiles(3, 40), tiles(40), tiles(40),
            tiles(3, 10), tiles(3, 10), tiles(24), tiles(7, 3), tiles(24), tiles(40), tiles(40),
            pltpu.SemaphoreType.DMA((40,)),
            pltpu.SemaphoreType.DMA((40,)),
        ],
        compiler_params=pltpu.CompilerParams(
            collective_id=0, has_side_effects=True, vmem_limit_bytes=40 * 1024 * 1024
        ),
        name="reduce",
    )(big, small)


def local(
    fine_points, parent, patch_count, qkv_fine, out_fine, pool_weight, qkv_coarse, out_coarse,
    cotangent,
):
    pts = lax.axis_index("pts")
    position = lax.axis_index("rep") * lax.axis_size("pts") + pts
    core = (pts % 2).reshape(1)
    swap = [(i, i ^ 1) for i in range(32)]
    far_cot = lax.ppermute(cotangent, "pts", swap)
    offset = (parent - position * 256).reshape(1, 1024)
    ab = fine_call(patch_count, offset, fine_points, qkv_fine, out_fine)
    arrived = lax.ppermute(ab[256:], "pts", [(i, i + 1) for i in range(31)])
    coarse_in = pl.pallas_call(
        coarse_in_kernel,
        out_shape=jax.ShapeDtypeStruct((256, 512), BF),
        in_specs=[VM, VM, VM],
        out_specs=VM,
        name="coarse_in",
    )(ab, arrived, pool_weight)
    far_in = lax.ppermute(coarse_in, "pts", swap)
    dn, mixed, big = coarse_call(core, coarse_in, far_in, cotangent, far_cot, qkv_coarse, out_coarse)
    far_dn, far_mixed = lax.ppermute((dn[256:], mixed[256:]), "pts", swap)
    coarse_out, small = pl.pallas_call(
        finish_kernel,
        out_shape=(
            jax.ShapeDtypeStruct((256, 512), BF),
            jax.ShapeDtypeStruct((2, 48, 16, 128), BF),
        ),
        in_specs=[SM] + [VM] * 10,
        out_specs=(VM, VM),
        name="finish",
    )(core, ab, arrived, pool_weight, coarse_in, cotangent, dn, far_dn, mixed, far_mixed, out_coarse)
    grads = reduce_call(big, small)
    return (coarse_out, *grads)


def solution(mesh):
    rows = P(("rep", "pts"), None)
    flat = P(("rep", "pts"))
    return jax.shard_map(
        local,
        mesh=mesh,
        in_specs=(rows, flat, flat, P(), P(), P(), P(), P(), rows),
        out_specs=(rows, P(), P(), P(), P()),
        check_vma=False,
    )
```

time: 498 us -> 141 us (0.28)
  matrix products: 211 us -> 0 us
  waiting for transfers between devices: 130 us -> 4.08 us
  Pallas kernels: 0 us -> 117 us
  blocking collectives: 51.1 us -> 0 us
  local copies, waits for them, and re-layouts: 47.2 us -> 9.76 us
  starting transfers between devices: 25.9 us -> 7.22 us
  between operations: 15.3 us -> 1.4 us
  other arithmetic: 14.2 us -> 1.28 us
    dot_general x57 -> x0, matrix products: 139 us -> none  [the longest x28 72.8 us: one_group(): jnp.einsum('yex,xyb->eyb', attention_weight, grouped_value_rows, preferre...]
    pallas_call x0 -> x5, Pallas kernels: none -> 117 us  [the longest x1 54.7 us: reduce_call(): pl.pallas_call(reduce_kernel, out_shape=(jax.ShapeDtypeStruct((256, 256),...]
    reduce_scatter x1 -> x0, waiting for transfers between devices: 105 us -> none  [sum_together(): lax.psum_scatter(lines, axis, tiled=True).reshape(-1)]
    sub x20 -> x0, matrix products: 72.5 us -> none  [one_group(): logit_table - lax.stop_gradient(jnp.max(logit_table, axis=-1, keepdims=Tr...]
    all_gather x1 -> x0, blocking collectives: 51.1 us -> none  [sent_together(): lax.all_gather(both, axis, axis=dim, tiled=True)]
    all_to_all x4 -> x0, waiting for transfers between devices: 20.9 us -> none  [copy_for_each(): return lax.all_to_all(copies, axis, split_axis=0, concat_axis=0, tiled=True)]
    all_to_all x4 -> x0, starting transfers between devices: 14.2 us -> none  [copy_for_each(): return lax.all_to_all(copies, axis, split_axis=0, concat_axis=0, tiled=True)]
    squeeze x16 -> x0, local copies, waits for them, and re-layouts: 13.3 us -> none  [attend(): mixed_rows = lax.map(one_group, (head_query, head_key, head_value))]
  transfers between devices with their start and end apart: 13 -> 5, of which waited for: 7 -> 3; matrix products, arithmetic and copies ran while one was open for 25% -> 1% of each run, Pallas kernels for 0% -> 2%
where the time goes in v1:
time: 141 us
  Pallas kernels  117 us (83%)
  local copies, waits for them, and re-layouts  9.76 us (7%)
  starting transfers between devices  7.22 us (5%)
  waiting for transfers between devices  4.08 us (3%)
    pallas_call x1, Pallas kernels, reduce_call(): pl.pallas_call(reduce_kernel, out_shape=(jax.ShapeDtypeStruct((256, 256),...  54.7 us
    pallas_call x1, Pallas kernels, fine_call(): pl.pallas_call(fine_kernel, out_shape=jax.ShapeDtypeStruct((288, 640), F3...  32.4 us
    pallas_call x1, Pallas kernels, coarse_call(): pl.pallas_call(coarse_kernel, out_shape=(jax.ShapeDtypeStruct((512, 512),...  23.8 us
    unnamed x20, local copies, waits for them, and re-layouts  6.98 us
    ppermute x1, starting transfers between devices, local(): arrived = lax.ppermute(ab[256:], 'pts', [(i, i + 1) for i in range(31)])  6.26 us
    pallas_call x1, Pallas kernels, local(): pl.pallas_call(finish_kernel, out_shape=(jax.ShapeDtypeStruct((256, 512),...  3.88 us
  transfers between devices with their start and end apart: 5, of which 3 were waited for; matrix products, arithmetic and copies ran while one was open for 1% of the time, Pallas kernels for 2%

profile of v1, /device:TPU:1, one launch (start us, length us, event | category | flops | bytes accessed | tf_op | source)
XLA Modules:
  0.0 140.9 jit_solution(5966902047200796072)
XLA Ops:
  0.6 0.0 copy-start.2
  1.3 1.3 broadcast_subtract_fusion
  2.6 32.4 %fine.1.ab_ref = f32[288,640]{1,0:T(8,128)} custom-call(s32[1]{0:T(128)S(6)} %copy.18.cnt_ref, s32[1,1024]{1,0:T(1,128)} %bitcast.2, bf16[1024,256]{1,0:T(8,128)(2,1)} %x_ref.1, bf16[256,768]{1,0:T(8,128)(2,1)} %w_ref.2, bf16[256,256]{1,0:T(8,128)(2,1)} %ow_ref.3), custom_call_target="tpu_custom_call" | custom-call | tf_op jit(solution)/shard_map/fine/pallas_call | solution.py:113
  35.1 0.9 slice.12
  35.9 6.3 %collective-permute-start = (f32[32,640]{1,0:T(8,128)S(1)}, f32[32,640]{1,0:T(8,128)S(1)}, u32[]{:S(2)}, u32[]{:S(2)}) collective-permute-start(f32[32,640]{1,0:T(8,128)S(1)} %slice.12), channel_id=1, source_target_pairs={{0,1},{1,2},{2,3},{3,4},{4,5},{5,6},{6,7},{7,8},{8,9},{9,10},{10,1... | collective-permute-start | bytes 245768 | tf_op jit(solution)/shard_map/ppermute | solution.py:446
  42.2 0.0 copy-done.2
  42.2 0.1 collective-permute-start.2
  42.3 1.4 collective-permute-done.arr_ref
  43.7 0.0 copy-start.3
  43.7 0.6 copy-done.3
  44.3 2.3 %coarse_in.1.c_ref = bf16[256,512]{1,0:T(8,128)(2,1)} custom-call(f32[288,640]{1,0:T(8,128)} %fine.1.ab_ref, f32[32,640]{1,0:T(8,128)} %copy-done.3, bf16[256,512]{1,0:T(8,128)(2,1)} %pw_ref.3), custom_call_target="tpu_custom_call" | custom-call | tf_op jit(solution)/shard_map/coarse_in/pallas_call | solution.py:447
  46.7 0.0 collective-permute-start.1
  46.7 0.0 collective-permute-done.2.ctf_ref
  46.7 0.0 copy-start.4
  46.7 1.7 %collective-permute-done.1.cf_ref = bf16[256,512]{1,0:T(8,128)(2,1)S(1)} collective-permute-done((bf16[256,512]{1,0:T(8,128)(2,1)}, bf16[256,512]{1,0:T(8,128)(2,1)S(1)}, u32[]{:S(2)}, u32[]{:S(2)}) %collective-permute-start.1) | collective-permute-done | bytes 262176 | tf_op jit(solution)/shard_map/ppermute | solution.py:454
  48.4 0.0 copy-start.5
  48.4 0.0 copy-done.4
  48.4 0.7 copy-done.5
  49.1 23.8 %coarse.1 = (bf16[512,512]{1,0:T(8,128)(2,1)}, bf16[512,256]{1,0:T(8,128)(2,1)}, bf16[256,16,128]{2,1,0:T(8,128)(2,1)}) custom-call(s32[1]{0:T(128)} %bitcast.core_ref, bf16[256,512]{1,0:T(8,128)(2,1)} %coarse_in.1.c_ref, bf16[256,512]{1,0:T(8,128)(2,1)} %copy-done.5, bf16[256,512]{1,0:T(8,128)(2,1)} %ct_ref.3, bf16[256,512]{1,0:T(8,128)(2,1)} %copy-done.4, ...), custom_call_target="tpu_custom_call" | custom-call | tf_op jit(solution)/shard_map/coarse/pallas_call | solution.py:229
  72.9 1.0 slice.10
  73.8 0.2 collective-permute-start.3
  74.0 0.9 slice.11
  75.0 0.0 copy-start
  75.0 0.7 collective-permute-start.4
  75.6 1.0 collective-permute-done.4.mixf_ref
  76.6 0.0 copy-start.7
  76.6 0.0 collective-permute-done.3.dnf_ref
  76.6 0.6 copy-done.7
  77.3 0.0 copy-start.6
  77.3 0.7 copy-done.6
  78.0 3.9 %finish.1 = (bf16[256,512]{1,0:T(8,128)(2,1)}, bf16[2,48,16,128]{3,2,1,0:T(8,128)(2,1)}) custom-call(s32[1]{0:T(128)} %bitcast.core_ref, f32[288,640]{1,0:T(8,128)} %fine.1.ab_ref, f32[32,640]{1,0:T(8,128)} %copy-done.3, bf16[256,512]{1,0:T(8,128)(2,1)} %pw_ref.3, bf16[256,512]{1,0:T(8,128)(2,1)} %coarse_in.1.c_ref, bf16[256,512]{1,0:T(8,128)(2,1)} %ct_ref.3, ...), custom_call_target="tpu_custom_call" | custom-call | tf_op jit(solution)/shard_map/finish/pallas_call | solution.py:457
  81.9 0.0 copy-done
  81.9 0.0 copy-start.1
  81.9 1.0 copy-done.1
  82.9 54.7 %reduce.1 = (bf16[256,256]{1,0:T(8,128)(2,1)S(1)}, bf16[256,512]{1,0:T(8,128)(2,1)S(1)}, bf16[512,1536]{1,0:T(8,128)(2,1)S(1)}, bf16[512,512]{1,0:T(8,128)(2,1)S(1)}) custom-call(bf16[256,16,128]{2,1,0:T(8,128)(2,1)S(1)} %copy-done, bf16[2,48,16,128]{3,2,1,0:T(8,128)(2,1)S(1)} %copy-done.1), custom_call_target="tpu_custom_call" | custom-call | tf_op jit(solution)/shard_map/reduce/pallas_call | solution.py:412
  137.6 0.7 copy.19
  138.3 0.7 copy.20
  139.0 1.1 copy.21
  140.1 0.8 copy.22
Async XLA Ops:
  0.6 41.6 %copy-start.2 = (bf16[256,512]{1,0:T(8,128)(2,1)S(1)}, bf16[256,512]{1,0:T(8,128)(2,1)}, u32[]{:S(2)}) copy-start(bf16[256,512]{1,0:T(8,128)(2,1)} %ct_ref.3) | copy-start | bytes 786436
  35.9 7.7 %collective-permute-start = (f32[32,640]{1,0:T(8,128)S(1)}, f32[32,640]{1,0:T(8,128)S(1)}, u32[]{:S(2)}, u32[]{:S(2)}) collective-permute-start(f32[32,640]{1,0:T(8,128)S(1)} %slice.12), channel_id=1, source_target_pairs={{0,1},{1,2},{2,3},{3,4},{4,5},{5,6},{6,7},{7,8},{8,9},{9,10},{10,1... | collective-permute-start | bytes 245768 | tf_op jit(solution)/shard_map/ppermute | solution.py:446
  42.2 4.4 %collective-permute-start.2 = (bf16[256,512]{1,0:T(8,128)(2,1)S(1)}, bf16[256,512]{1,0:T(8,128)(2,1)S(1)}, u32[]{:S(2)}, u32[]{:S(2)}) collective-permute-start(bf16[256,512]{1,0:T(8,128)(2,1)S(1)} %copy-done.2), channel_id=1, source_target_pairs={{0,1},{1,0},{2,3},{3,2},{4,5},{5,4},{6,7},{7,6},{8,9},{9,8},{10,11... | collective-permute-start | bytes 786440 | tf_op jit(solution)/shard_map/ppermute | solution.py:443
  43.7 0.6 copy-start.3
  46.7 1.7 %collective-permute-start.1 = (bf16[256,512]{1,0:T(8,128)(2,1)}, bf16[256,512]{1,0:T(8,128)(2,1)S(1)}, u32[]{:S(2)}, u32[]{:S(2)}) collective-permute-start(bf16[256,512]{1,0:T(8,128)(2,1)} %coarse_in.1.c_ref), channel_id=1, source_target_pairs={{0,1},{1,0},{2,3},{3,2},{4,5},{5,4},{6,7},{7,6},{8,9},{9,8},{10,11... | collective-permute-start | bytes 786440 | tf_op jit(solution)/shard_map/ppermute | solution.py:454
  46.7 1.7 %copy-start.4 = (bf16[256,512]{1,0:T(8,128)(2,1)}, bf16[256,512]{1,0:T(8,128)(2,1)S(1)}, u32[]{:S(2)}) copy-start(bf16[256,512]{1,0:T(8,128)(2,1)S(1)} %collective-permute-done.2.ctf_ref) | copy-start | bytes 786436
  48.4 0.7 copy-start.5
  73.8 2.8 %collective-permute-start.3 = (bf16[256,512]{1,0:T(8,128)(2,1)S(1)}, bf16[256,512]{1,0:T(8,128)(2,1)S(1)}, u32[]{:S(2)}, u32[]{:S(2)}) collective-permute-start(bf16[256,512]{1,0:T(8,128)(2,1)S(1)} %slice.10), channel_id=1, source_target_pairs={{0,1},{1,0},{2,3},{3,2},{4,5},{5,4},{6,7},{7,6},{8,9},{9,8},{10,11... | collective-permute-start | bytes 786440 | tf_op jit(solution)/shard_map/ppermute | solution.py:456
  75.0 6.9 %copy-start = (bf16[256,16,128]{2,1,0:T(8,128)(2,1)S(1)}, bf16[256,16,128]{2,1,0:T(8,128)(2,1)}, u32[]{:S(2)}) copy-start(bf16[256,16,128]{2,1,0:T(8,128)(2,1)} %get-tuple-element.17.big_ref) | copy-start | bytes 3145732
  75.0 1.6 %collective-permute-start.4 = (bf16[256,256]{1,0:T(8,128)(2,1)S(1)}, bf16[256,256]{1,0:T(8,128)(2,1)S(1)}, u32[]{:S(2)}, u32[]{:S(2)}) collective-permute-start(bf16[256,256]{1,0:T(8,128)(2,1)S(1)} %slice.11), channel_id=1, source_target_pairs={{0,1},{1,0},{2,3},{3,2},{4,5},{5,4},{6,7},{7,6},{8,9},{9,8},{10,11... | collective-permute-start | bytes 393224 | tf_op jit(solution)/shard_map/ppermute | solution.py:456
  76.6 0.7 copy-start.7
  77.3 0.7 copy-start.6
  81.9 1.0 copy-start.1

commit v2 on v1

v2 whole, which is shorter than its diff:
```python
import jax
import jax.numpy as jnp
from jax import lax
from jax.experimental import pallas as pl
from jax.experimental.pallas import tpu as pltpu
from jax.sharding import PartitionSpec as P

F32 = jnp.float32
BF = jnp.bfloat16
EPS = 1e-6
LOG2E = 1.4426950408889634
LN2 = 0.6931471805599453
SAFE = 80.0
MESH = pl.DeviceIdType.MESH
VM = pl.BlockSpec(memory_space=pltpu.VMEM)
SM = pl.BlockSpec(memory_space=pltpu.SMEM)

NN = (((1,), (0,)), ((), ()))
NT = (((1,), (1,)), ((), ()))
TN = (((0,), (0,)), ((), ()))
TT = (((0,), (1,)), ((), ()))


def mm(a, b, dims=NN):
    return lax.dot_general(a, b, dims, preferred_element_type=F32)


def normalize(values):
    return values * lax.rsqrt(jnp.mean(values * values, axis=-1, keepdims=True) + EPS)


def split_dot(a, b):
    high = a.astype(BF)
    low = (a - high.astype(F32)).astype(BF)
    return mm(high, b) + mm(low, b)


def head_rows(rows, width):
    return lax.broadcasted_iota(jnp.int32, (rows, width), 0) // 16


def score_bound(qt, k):
    channels = qt.shape[0]
    heads = (
        lax.broadcasted_iota(jnp.int32, (channels, 128), 0) // 16
        == lax.broadcasted_iota(jnp.int32, (channels, 128), 1)
    ).astype(BF)
    kf = k.astype(F32)
    k2 = mm((kf * kf).astype(BF), heads)
    q = qt.astype(F32)
    q2 = (q * q).reshape(channels // 16, 16, qt.shape[1]).sum(axis=1)
    return jnp.max(q2) * jnp.max(k2)


def fine_kernel(cnt_ref, off_ref, x_ref, w_ref, ow_ref, ab_ref, k_ref, qt_ref, va_ref, mt_ref):
    count = cnt_ref[0]
    x = x_ref[...]
    n = normalize(x.astype(F32)).astype(BF)
    k_ref[...] = mm(n, w_ref[:, 256:512]).astype(BF)
    qt_ref[...] = (mm(w_ref[:, :256], n, TT) * (0.25 * LOG2E)).astype(BF)
    vt = mm(w_ref[:, 512:], n, TT).astype(BF)
    live = lax.broadcasted_iota(jnp.int32, (1, 1024), 1) < count
    ones = jnp.where(jnp.broadcast_to(live, (16, 1024)), 1.0, 0.0).astype(BF)
    for h in range(16):
        rows = vt[h * 16 : h * 16 + 16, :].astype(F32)
        va_ref[h, 0:16, :] = jnp.where(live, rows, 0.0).astype(BF)
        va_ref[h, 16:32, :] = ones
    bound = score_bound(qt_ref[...], k_ref[...])
    quick = bound < SAFE * SAFE

    def safe_head(h, carry):
        half = pl.multiple_of((h // 8) * 128, 128)
        row = pl.multiple_of(h * 16, 16)
        chosen = head_rows(128, 256) == h % 8
        alive = lax.broadcasted_iota(jnp.int32, (1024, 256), 0) < count
        for t in range(4):
            cols = slice(t * 256, t * 256 + 256)
            part = qt_ref[pl.ds(half, 128), cols]
            s = mm(k_ref[:, pl.ds(half, 128)], jnp.where(chosen, part, jnp.zeros_like(part)))
            s = jnp.where(alive, s, -1e30)
            s = s - jnp.max(s, axis=0, keepdims=True)
            o = mm(va_ref[h], jnp.exp2(s).astype(BF))
            mt_ref[pl.ds(row, 16), cols] = (o[:16] / o[16:]).astype(BF)
        return carry

    def quick_head(h, carry):
        half = pl.multiple_of((h // 8) * 128, 128)
        row = pl.multiple_of(h * 16, 16)
        ck, cq = 1024, 256
        units = [(t, c) for t in range(1024 // cq) for c in range(1024 // ck)]
        chosen = head_rows(128, cq) == h % 8
        scores, weights, sums, queries = {}, {}, {}, {}
        for i in range(len(units) + 2):
            if i < len(units):
                t, c = units[i]
                if c == 0:
                    part = qt_ref[pl.ds(half, 128), t * cq : t * cq + cq]
                    queries[t] = jnp.where(chosen, part, jnp.zeros_like(part))
                scores[i] = mm(k_ref[c * ck : c * ck + ck, pl.ds(half, 128)], queries[t])
            if 1 <= i <= len(units):
                weights[i - 1] = jnp.exp2(scores.pop(i - 1)).astype(BF)
            if i >= 2:
                t, c = units[i - 2]
                o = mm(va_ref[h, :, c * ck : c * ck + ck], weights.pop(i - 2))
                sums[t] = o if c == 0 else sums[t] + o
                if c == 1024 // ck - 1:
                    o = sums.pop(t)
                    mt_ref[pl.ds(row, 16), t * cq : t * cq + cq] = (o[:16] / o[16:]).astype(BF)
        return carry

    @pl.when(quick)
    def _():
        lax.fori_loop(0, 16, quick_head, 0, unroll=4)

    @pl.when(jnp.logical_not(quick))
    def _():
        lax.fori_loop(0, 16, safe_head, 0)

    table = jnp.where(
        (lax.broadcasted_iota(jnp.int32, (288, 1024), 0) == off_ref[...]) & live, 1.0, 0.0
    )
    total = jnp.sum(table, axis=1, keepdims=True)
    table = table.astype(BF)
    b = mm(table, mt_ref[...], NT)
    ab_ref[:, :256] = mm(table, x) + split_dot(b, ow_ref[...])
    ab_ref[:, 256:512] = b
    ab_ref[:, 512:] = jnp.broadcast_to(total, (288, 128))


def fine_call(count, offset, x, w, ow):
    return pl.pallas_call(
        fine_kernel,
        out_shape=jax.ShapeDtypeStruct((288, 640), F32),
        in_specs=[SM, VM, VM, VM, VM],
        out_specs=VM,
        scratch_shapes=[
            pltpu.VMEM((1024, 256), BF),
            pltpu.VMEM((256, 1024), BF),
            pltpu.VMEM((16, 32, 1024), BF),
            pltpu.VMEM((256, 1024), BF),
        ],
        compiler_params=pltpu.CompilerParams(vmem_limit_bytes=56 * 1024 * 1024),
        name="fine",
    )(count, offset, x, w, ow)


def pooled(ab_ref, arr_ref, first, last):
    top = ab_ref[:32, first:last] + arr_ref[:, first:last]
    return jnp.concatenate([top, ab_ref[32:256, first:last]], axis=0)


def pooled_mean(ab_ref, arr_ref, pw_ref):
    a = pooled(ab_ref, arr_ref, 0, 256)
    count = jnp.maximum(pooled(ab_ref, arr_ref, 512, 640)[:, :1], 1.0)
    return split_dot(a, pw_ref[...]) / count, count


GA = 0.7978845608028654
GB = 0.044715


def coarse_in_kernel(ab_ref, arr_ref, pw_ref, c_ref):
    u, _ = pooled_mean(ab_ref, arr_ref, pw_ref)
    c_ref[...] = (0.5 * u * (1.0 + jnp.tanh(GA * (u + GB * u * u * u)))).astype(BF)


def coarse_kernel(
    core_ref, c_ref, cf_ref, ct_ref, ctf_ref, w_ref, ow_ref,
    dn_ref, mix_ref, g_ref,
    n_ref, cot_ref, k_ref, v_ref, kt_ref, qt_ref, va_ref, dot_ref, ot_ref, dp_ref,
    p_ref, pb_ref, ds_ref,
):
    core = core_ref[0]
    lo = pl.multiple_of(core * 256, 256)
    n_ref[:256] = normalize(c_ref[...].astype(F32)).astype(BF)
    n_ref[256:] = normalize(cf_ref[...].astype(F32)).astype(BF)
    cot_ref[:256] = ct_ref[...]
    cot_ref[256:] = ctf_ref[...]
    n = n_ref[...]
    wq = w_ref[:, pl.ds(lo, 256)]
    wk = w_ref[:, pl.ds(512 + lo, 256)]
    wv = w_ref[:, pl.ds(1024 + lo, 256)]
    qt_ref[...] = (mm(wq, n, TT) * (0.25 * LOG2E)).astype(BF)
    k_ref[...] = mm(n, wk).astype(BF)
    v_ref[...] = mm(n, wv).astype(BF)
    kt_ref[...] = mm(wk, n, TT).astype(BF)
    vt = mm(wv, n, TT).astype(BF)
    for h in range(16):
        va_ref[h, :16, :] = vt[h * 16 : h * 16 + 16, :]
        va_ref[h, 16:, :] = jnp.ones((16, 512), BF)
    dot_ref[...] = mm(ow_ref[pl.ds(lo, 256), :], cot_ref[...], NT)
    quick = score_bound(qt_ref[...], k_ref[...]) < SAFE * SAFE

    def stage_one(h, slot, shift):
        half = pl.multiple_of((h // 8) * 128, 128)
        row = pl.multiple_of(h * 16, 16)
        chosen = head_rows(128, 512) == h % 8
        part = qt_ref[pl.ds(half, 128), :]
        qm = jnp.where(chosen, part, jnp.zeros_like(part))
        s = mm(k_ref[:, pl.ds(half, 128)], qm)
        if shift:
            s = s - jnp.max(s, axis=0, keepdims=True)
        p = jnp.exp2(s)
        p_ref[slot] = p
        pb_ref[slot] = p.astype(BF)

    def stage_two(h, slot):
        half = pl.multiple_of((h // 8) * 128, 128)
        row = pl.multiple_of(h * 16, 16)
        chosen = head_rows(128, 512) == h % 8
        pb = pb_ref[slot]
        o = mm(va_ref[h], pb)
        inverse = 1.0 / o[16:]
        on = o[:16] * inverse
        ot_ref[pl.ds(row, 16), :] = on.astype(BF)
        do = dot_ref[pl.ds(row, 16), :] * inverse
        dob = do.astype(BF)
        delta = jnp.sum(dob.astype(F32) * on, axis=0, keepdims=True)
        tiled = jnp.concatenate([dob] * 8, axis=0)
        dom = jnp.where(chosen, tiled, jnp.zeros_like(tiled))
        dpt = mm(v_ref[:, pl.ds(half, 128)], dom)
        ds_ref[slot] = (p_ref[slot] * (dpt - delta)).astype(BF)
        dp_ref[pl.ds(512 + row, 16), :] = mm(dob, pb, NT).astype(BF)

    def stage_three(h, slot):
        row = pl.multiple_of(h * 16, 16)
        ds = ds_ref[slot]
        dp_ref[pl.ds(row, 16), :] = (mm(kt_ref[pl.ds(row, 16), :], ds) * 0.25).astype(BF)
        dk = mm(qt_ref[pl.ds(row, 16), :], ds, NT) * LN2
        dp_ref[pl.ds(256 + row, 16), :] = dk.astype(BF)

    def attend(shift):
        stage_one(0, 0, shift)
        stage_one(1, 1, shift)
        stage_two(0, 0)

        def step(j, carry):
            for e in (0, 1):
                h = 2 * j + e
                stage_two(h + 1, 1 - e)
                stage_three(h, e)
                stage_one(h + 2, e, shift)
            return carry

        lax.fori_loop(0, 7, step, 0)
        stage_two(15, 1)
        stage_three(14, 0)
        stage_three(15, 1)

    @pl.when(quick)
    def _():
        attend(False)

    @pl.when(jnp.logical_not(quick))
    def _():
        attend(True)

    mix_ref[...] = jnp.transpose(ot_ref[...])
    dnt = (
        mm(wq, dp_ref[:256, :]) + mm(wk, dp_ref[256:512, :]) + mm(wv, dp_ref[512:, :])
    ).astype(BF)
    dn_ref[...] = jnp.transpose(dnt)
    nt = jnp.transpose(n_ref[...])
    for j in range(6):
        block = mm(nt, dp_ref[j * 128 : j * 128 + 128, :], NT).astype(BF)
        g_ref[j * 32 : j * 32 + 32] = block.reshape(32, 16, 128)
    for j in range(4):
        block = mm(ot_ref[...], cot_ref[:, j * 128 : j * 128 + 128]).astype(BF)
        g_ref[192 + j * 16 : 208 + j * 16] = block.reshape(16, 16, 128)


def coarse_call(core, c, cf, ct, ctf, w, ow):
    return pl.pallas_call(
        coarse_kernel,
        out_shape=(
            jax.ShapeDtypeStruct((512, 512), BF),
            jax.ShapeDtypeStruct((512, 256), BF),
            jax.ShapeDtypeStruct((256, 16, 128), BF),
        ),
        in_specs=[SM, VM, VM, VM, VM, VM, VM],
        out_specs=(VM, VM, VM),
        scratch_shapes=[
            pltpu.VMEM((512, 512), BF),
            pltpu.VMEM((512, 512), BF),
            pltpu.VMEM((512, 256), BF),
            pltpu.VMEM((512, 256), BF),
            pltpu.VMEM((256, 512), BF),
            pltpu.VMEM((256, 512), BF),
            pltpu.VMEM((16, 32, 512), BF),
            pltpu.VMEM((256, 512), F32),
            pltpu.VMEM((256, 512), BF),
            pltpu.VMEM((768, 512), BF),
            pltpu.VMEM((2, 512, 512), F32),
            pltpu.VMEM((2, 512, 512), BF),
            pltpu.VMEM((2, 512, 512), BF),
        ],
        compiler_params=pltpu.CompilerParams(vmem_limit_bytes=56 * 1024 * 1024),
        name="coarse",
    )(core, c, cf, ct, ctf, w, ow)


def other_one(v):
    return v + 1 - 2 * (v % 2)


def other_two(v):
    return 3 - v


def tail_kernel(
    ab_ref, arr_ref, pw_ref, c_ref, ct_ref, dn_ref, mix_ref, ow_ref, big,
    out_ref, gof_ref, gp_ref, gq_ref, goc_ref,
    dnf, mixf, small, sm, g, r1, s1, r2, ra, rb, ha, hb, ra2, rb2, z, rz, zf, fa, fb, full,
    send, recv,
):
    rep = lax.axis_index("rep")
    pts = lax.axis_index("pts")
    x = rep % 4
    zlo = rep // 4
    y = pts // 8
    zhi = (pts // 2) % 4
    core = pts % 2
    zi = zhi * 2 + zlo

    def at_x(v):
        return (zlo * 4 + v, pts)

    def at_y(v):
        return (rep, v * 8 + zhi * 2 + core)

    def at_z(v):
        return ((v % 2) * 4 + x, y * 8 + (v // 2) * 2 + core)

    partner = (rep, pts + 1 - 2 * core)
    barrier = pltpu.get_barrier_semaphore()
    peers = [partner]
    peers += [at_x((x + d) % 4) for d in (1, 2, 3)] + [at_y((y + d) % 4) for d in (1, 2, 3)]
    peers += [at_z((zi + d) % 8) for d in range(1, 8)]
    for peer in peers:
        pl.semaphore_signal(barrier, inc=1, device_id=peer, device_id_type=MESH)
    pl.semaphore_wait(barrier, len(peers))

    counter = [0]

    def push(src, dst, peer):
        i = counter[0]
        counter[0] += 1
        copy = pltpu.make_async_remote_copy(
            src_ref=src, dst_ref=dst, send_sem=send.at[i], recv_sem=recv.at[i],
            device_id=peer, device_id_type=MESH,
        )
        copy.start()
        return copy

    def wait(copies):
        for copy in copies:
            copy.wait()

    streams = [
        (x, at_x, 0, other_one, other_two),
        (x, at_x, 64, other_two, other_one),
        (y, at_y, 128, other_one, other_two),
        (y, at_y, 192, other_two, other_one),
    ]

    def quarter(base, v):
        return pl.ds(base + v * 16, 16)

    trade = [push(dn_ref.at[pl.ds(256, 256)], dnf, partner)]
    trade.append(push(mix_ref.at[pl.ds(256, 256)], mixf, partner))
    first = []
    for k, (v, place, base, one, two) in enumerate(streams):
        p = one(v)
        first.append(push(big.at[quarter(base, two(p))], r1.at[k, 1], place(p)))
        first.append(push(big.at[quarter(base, p)], r1.at[k, 0], place(p)))

    c = c_ref[...].astype(F32)
    u, count = pooled_mean(ab_ref, arr_ref, pw_ref)
    th = jnp.tanh(GA * (u + GB * u * u * u))
    slope = 0.5 * (1.0 + th) + 0.5 * u * (1.0 - th * th) * (GA * (1.0 + 3.0 * GB * u * u))
    r = lax.rsqrt(jnp.mean(c * c, axis=-1, keepdims=True) + EPS)
    at = jnp.transpose(pooled(ab_ref, arr_ref, 0, 256)).astype(BF)
    bt = jnp.transpose(pooled(ab_ref, arr_ref, 256, 512)).astype(BF)
    wait(trade)
    dn = dn_ref[:256].astype(F32) + dnf[...].astype(F32)
    inner = jnp.mean(dn * c, axis=-1, keepdims=True)
    dc = r * dn - c * (r * r * r * inner) + ct_ref[...].astype(F32)
    gs = (slope * dc / count).astype(BF)
    gw = mm(gs, pw_ref[...], NT).astype(BF)
    for half in range(2):
        rows = slice(half * 128, half * 128 + 128)
        for j in range(4):
            block = mm(at[rows], gs[:, j * 128 : j * 128 + 128]).astype(BF)
            small[half, j * 8 : j * 8 + 8] = block.reshape(8, 16, 128)
        for j in range(2):
            block = mm(bt[rows], gw[:, j * 128 : j * 128 + 128]).astype(BF)
            small[half, 32 + j * 8 : 40 + j * 8] = block.reshape(8, 16, 128)
    swap = push(small.at[1 - core], sm, partner)

    def f32(value):
        return value.astype(F32)

    second = []
    for k, (v, place, base, one, two) in enumerate(streams):
        wait(first[2 * k : 2 * k + 2])
        s1[k] = (f32(big[quarter(base, two(v))]) + f32(r1[k, 1])).astype(BF)
        second.append(push(s1.at[k], r2.at[k], place(two(v))))
    swap.wait()
    g[:48] = (f32(small[core]) + f32(sm[...])).astype(BF)
    g[48:] = jnp.zeros((16, 16, 128), BF)
    third = []
    for d in (1, 2, 3):
        to = (x + d) % 4
        third.append(push(g.at[pl.ds(to * 8, 8)], ra.at[d - 1], at_x(to)))
        to = (y + d) % 4
        third.append(push(g.at[pl.ds(32 + to * 8, 8)], rb.at[d - 1], at_y(to)))
    lo = pl.multiple_of(core * 256, 256)
    hi = pl.multiple_of(256 - core * 256, 256)
    mixed = mm(mix_ref[:256], ow_ref[pl.ds(lo, 256), :]) + mm(mixf[...], ow_ref[pl.ds(hi, 256), :])
    out_ref[...] = (c + mixed).astype(BF)

    def add(own, slots, n):
        total = f32(own)
        for d in range(n):
            total = total + f32(slots[d])
        return total.astype(BF)

    for k, (v, place, base, one, two) in enumerate(streams):
        second[k].wait()
        total = (f32(big[quarter(base, v)]) + f32(r1[k, 0]) + f32(r2[k])).astype(BF)
        keep = ha if k < 2 else hb
        spot = (k % 2) * 4
        keep[:, spot : spot + 4] = total.reshape(4, 4, 16, 128)
    wait(third)
    ha[:, 8:] = add(g[pl.ds(x * 8, 8)], ra, 3).reshape(4, 2, 16, 128)
    hb[:, 8:] = add(g[pl.ds(32 + y * 8, 8)], rb, 3).reshape(4, 2, 16, 128)
    moves = []
    for d in (1, 2, 3):
        to = (y + d) % 4
        moves.append(push(ha.at[to], ra2.at[d - 1], at_y(to)))
        to = (x + d) % 4
        moves.append(push(hb.at[to], rb2.at[d - 1], at_x(to)))
    wait(moves)
    z[:10] = add(ha[y], ra2, 3)
    z[10:20] = add(hb[x], rb2, 3)
    z[20:] = jnp.zeros((4, 16, 128), BF)
    moves = []
    for d in (4, 3, 5, 2, 6, 1, 7):
        to = (zi + d) % 8
        moves.append(push(z.at[pl.ds(to * 3, 3)], rz.at[d - 1], at_z(to)))
    wait(moves)
    mine = pl.ds(zi * 3, 3)
    zf[mine] = add(z[mine], rz, 7)
    wait([push(zf.at[mine], zf.at[mine], at_z((zi + d) % 8)) for d in (4, 3, 5, 2, 6, 1, 7)])
    fa[y] = zf[:10]
    fb[x] = zf[10:20]
    moves = []
    for d in (1, 2, 3):
        moves.append(push(fa.at[y], fa.at[y], at_y((y + d) % 4)))
        moves.append(push(fb.at[x], fb.at[x], at_x((x + d) % 4)))
    wait(moves)

    def share(rows, peer):
        spot = full.at[core, rows]
        return push(spot, spot, peer)

    ups = []
    first, second, done = [], [], []
    for k, (v, place, base, one, two) in enumerate(streams):
        kept = fa if k < 2 else fb
        spot = (k % 2) * 4
        own = quarter(base, v)
        full[core, own] = kept[:, spot : spot + 4].reshape(16, 16, 128)
        first.append(share(own, place(two(v))))
        second.append(share(own, place(one(v))))
        done.append(share(own, partner))
    la, lb = pl.ds(256 + x * 8, 8), pl.ds(288 + y * 8, 8)
    full[core, la] = fa[:, 8:].reshape(8, 16, 128)
    full[core, lb] = fb[:, 8:].reshape(8, 16, 128)
    for d in (1, 2, 3):
        ups.append(share(la, at_x((x + d) % 4)))
        ups.append(share(lb, at_y((y + d) % 4)))
    for k, (v, place, base, one, two) in enumerate(streams):
        first[k].wait()
        came = quarter(base, two(v))
        second.append(share(came, place(one(v))))
        done.append(share(came, partner))
    wait(ups)
    done.append(share(pl.ds(256, 48), partner))
    for k, (v, place, base, one, two) in enumerate(streams):
        second[k].wait()
        second[4 + k].wait()
        done.append(share(quarter(base, one(v)), partner))
        done.append(share(quarter(base, two(one(v))), partner))
    wait(done)
    for c in range(2):
        for j in range(6):
            column = (j // 2) * 512 + c * 256 + (j % 2) * 128
            gq_ref[:, column : column + 128] = full[c, j * 32 : j * 32 + 32].reshape(512, 128)
        for j in range(4):
            rows = slice(c * 256, c * 256 + 256)
            tile = full[c, 192 + j * 16 : 208 + j * 16].reshape(256, 128)
            goc_ref[rows, j * 128 : j * 128 + 128] = tile
        rows = slice(c * 128, c * 128 + 128)
        for j in range(4):
            tile = full[c, 256 + j * 8 : 264 + j * 8].reshape(128, 128)
            gp_ref[rows, j * 128 : j * 128 + 128] = tile
        for j in range(2):
            tile = full[c, 288 + j * 8 : 296 + j * 8].reshape(128, 128)
            gof_ref[rows, j * 128 : j * 128 + 128] = tile


def tail_call(*operands):
    def tiles(*n):
        return pltpu.VMEM((*n, 16, 128), BF)

    return pl.pallas_call(
        tail_kernel,
        out_shape=(
            jax.ShapeDtypeStruct((256, 512), BF),
            jax.ShapeDtypeStruct((256, 256), BF),
            jax.ShapeDtypeStruct((256, 512), BF),
            jax.ShapeDtypeStruct((512, 1536), BF),
            jax.ShapeDtypeStruct((512, 512), BF),
        ),
        in_specs=[VM] * 9,
        out_specs=(VM,) * 5,
        scratch_shapes=[
            pltpu.VMEM((256, 512), BF), pltpu.VMEM((256, 256), BF),
            tiles(2, 48), tiles(48), tiles(64),
            tiles(4, 2, 16), tiles(4, 16), tiles(4, 16), tiles(3, 8), tiles(3, 8),
            tiles(4, 10), tiles(4, 10), tiles(3, 10), tiles(3, 10),
            tiles(24), tiles(7, 3), tiles(24), tiles(4, 10), tiles(4, 10), tiles(2, 320),
            pltpu.SemaphoreType.DMA((96,)),
            pltpu.SemaphoreType.DMA((96,)),
        ],
        compiler_params=pltpu.CompilerParams(
            collective_id=0, has_side_effects=True, vmem_limit_bytes=40 * 1024 * 1024
        ),
        name="tail",
    )(*operands)


def local(
    fine_points, parent, patch_count, qkv_fine, out_fine, pool_weight, qkv_coarse, out_coarse,
    cotangent,
):
    pts = lax.axis_index("pts")
    position = lax.axis_index("rep") * lax.axis_size("pts") + pts
    core = (pts % 2).reshape(1)
    swap = [(i, i ^ 1) for i in range(32)]
    far_cot = lax.ppermute(cotangent, "pts", swap)
    offset = (parent - position * 256).reshape(1, 1024)
    ab = fine_call(patch_count, offset, fine_points, qkv_fine, out_fine)
    arrived = lax.ppermute(ab[256:], "pts", [(i, i + 1) for i in range(31)])
    coarse_in = pl.pallas_call(
        coarse_in_kernel,
        out_shape=jax.ShapeDtypeStruct((256, 512), BF),
        in_specs=[VM, VM, VM],
        out_specs=VM,
        name="coarse_in",
    )(ab, arrived, pool_weight)
    far_in = lax.ppermute(coarse_in, "pts", swap)
    dn, mixed, big = coarse_call(core, coarse_in, far_in, cotangent, far_cot, qkv_coarse, out_coarse)
    return tail_call(
        ab, arrived, pool_weight, coarse_in, cotangent, dn, mixed, out_coarse, big
    )


def solution(mesh):
    rows = P(("rep", "pts"), None)
    flat = P(("rep", "pts"))
    return jax.shard_map(
        local,
        mesh=mesh,
        in_specs=(rows, flat, flat, P(), P(), P(), P(), P(), rows),
        out_specs=(rows, P(), P(), P(), P()),
        check_vma=False,
    )
```

time: 141 us -> 115 us (0.82)
  Pallas kernels: 117 us -> 93.4 us
    pallas_call x1, Pallas kernels: 32.4 us -> 17.9 us  [fine_call(): pl.pallas_call(fine_kernel, out_shape=jax.ShapeDtypeStruct((288, 640), F3...]
    pallas_call x2 -> x1, Pallas kernels: 58.6 us -> 52.2 us  [tail_call(): pl.pallas_call(tail_kernel, out_shape=(jax.ShapeDtypeStruct((256, 512), B...]
    pallas_call x1, Pallas kernels: 23.8 us -> 20.8 us  [coarse_call(): pl.pallas_call(coarse_kernel, out_shape=(jax.ShapeDtypeStruct((512, 512),...]
    slice x2 -> x0, local copies, waits for them, and re-layouts: 1.88 us -> none  [local(): far_dn, far_mixed = lax.ppermute((dn[256:], mixed[256:]), 'pts', swap)]
    unnamed x20 -> x31, local copies, waits for them, and re-layouts: 6.98 us -> 8.58 us
  transfers between devices with their start and end apart: 5 -> 3, of which waited for: 3 -> 2; matrix products, arithmetic and copies ran while one was open for 1% -> 0% of each run, Pallas kernels for 2% -> 2%
where the time goes in v2:
time: 115 us
  Pallas kernels  93.4 us (81%)
  local copies, waits for them, and re-layouts  9.47 us (8%)
  starting transfers between devices  6.35 us (6%)
  waiting for transfers between devices  3.09 us (3%)
  between operations  1.44 us (1%)
  other arithmetic  1.28 us (1%)
    pallas_call x1, Pallas kernels, tail_call(): pl.pallas_call(tail_kernel, out_shape=(jax.ShapeDtypeStruct((256, 512), B...  52.2 us
    pallas_call x1, Pallas kernels, coarse_call(): pl.pallas_call(coarse_kernel, out_shape=(jax.ShapeDtypeStruct((512, 512),...  20.8 us
    pallas_call x1, Pallas kernels, fine_call(): pl.pallas_call(fine_kernel, out_shape=jax.ShapeDtypeStruct((288, 640), F3...  17.9 us
    unnamed x31, local copies, waits for them, and re-layouts  8.58 us
    ppermute x1, starting transfers between devices, local(): arrived = lax.ppermute(ab[256:], 'pts', [(i, i + 1) for i in range(31)])  6.26 us
    pallas_call x1, Pallas kernels, local(): pl.pallas_call(coarse_in_kernel, out_shape=jax.ShapeDtypeStruct((256, 512...  2.35 us
  transfers between devices with their start and end apart: 3, of which 2 were waited for; matrix products, arithmetic and copies ran while one was open for 0% of the time, Pallas kernels for 2%

profile of v2, /device:TPU:1, one launch (start us, length us, event | category | flops | bytes accessed | tf_op | source)
XLA Modules:
  0.0 115.0 jit_solution(885838628047467693)
XLA Ops:
  0.6 0.0 copy-start.5
  1.3 1.3 %broadcast_subtract_fusion = s32[1024]{0:T(1024)} fusion(s32[1024]{0:T(1024)} %param.10, s32[]{:T(128)S(6)} %mul.7), kind=kLoop, calls=%fused_computation | loop fusion | flops 1024 | bytes 8196 | tf_op jit(solution)/shard_map/sub | solution.py:553
  2.6 17.9 %fine.1.ab_ref = f32[288,640]{1,0:T(8,128)} custom-call(s32[1]{0:T(128)S(6)} %copy.19.cnt_ref, s32[1,1024]{1,0:T(1,128)} %bitcast.2, bf16[1024,256]{1,0:T(8,128)(2,1)} %x_ref.1, bf16[256,768]{1,0:T(8,128)(2,1)} %w_ref.2, bf16[256,256]{1,0:T(8,128)(2,1)} %ow_ref.3), custom_call_target="tpu_custom_call" | custom-call | tf_op jit(solution)/shard_map/fine/pallas_call | solution.py:131
  20.6 0.9 slice.4
  21.5 6.3 %collective-permute-start = (f32[32,640]{1,0:T(8,128)S(1)}, f32[32,640]{1,0:T(8,128)S(1)}, u32[]{:S(2)}, u32[]{:S(2)}) collective-permute-start(f32[32,640]{1,0:T(8,128)S(1)} %slice.4), channel_id=1, source_target_pairs={{0,1},{1,2},{2,3},{3,4},{4,5},{5,6},{6,7},{7,8},{8,9},{9,10},{10,1... | collective-permute-start | bytes 245768 | tf_op jit(solution)/shard_map/ppermute | solution.py:555
  27.7 0.0 copy-done.5
  27.7 0.1 collective-permute-start.2
  27.8 1.4 %collective-permute-done.arr_ref = f32[32,640]{1,0:T(8,128)S(1)} collective-permute-done((f32[32,640]{1,0:T(8,128)S(1)}, f32[32,640]{1,0:T(8,128)S(1)}, u32[]{:S(2)}, u32[]{:S(2)}) %collective-permute-start) | collective-permute-done | bytes 81952 | tf_op jit(solution)/shard_map/ppermute | solution.py:555
  29.2 0.0 copy-start.8
  29.2 0.6 copy-done.8
  29.8 2.4 %coarse_in.1.c_ref = bf16[256,512]{1,0:T(8,128)(2,1)} custom-call(f32[288,640]{1,0:T(8,128)} %fine.1.ab_ref, f32[32,640]{1,0:T(8,128)} %copy-done.8, bf16[256,512]{1,0:T(8,128)(2,1)} %pw_ref.3), custom_call_target="tpu_custom_call" | custom-call | tf_op jit(solution)/shard_map/coarse_in/pallas_call | solution.py:556
  32.2 0.0 collective-permute-start.1
  32.2 0.0 collective-permute-done.2.ctf_ref
  32.2 0.0 copy-start.11
  32.2 1.7 %collective-permute-done.1.cf_ref = bf16[256,512]{1,0:T(8,128)(2,1)S(1)} collective-permute-done((bf16[256,512]{1,0:T(8,128)(2,1)}, bf16[256,512]{1,0:T(8,128)(2,1)S(1)}, u32[]{:S(2)}, u32[]{:S(2)}) %collective-permute-start.1) | collective-permute-done | bytes 262176 | tf_op jit(solution)/shard_map/ppermute | solution.py:563
  33.9 0.0 copy-start.12
  33.9 0.0 copy-done.11
  33.9 0.7 copy-done.12
  34.6 0.0 copy-start
  34.6 0.0 copy-start.1
  34.6 0.0 copy-start.2
  34.6 0.0 copy-start.4
  34.6 0.0 copy-start.6
  34.7 0.0 copy-start.9
  34.7 20.8 %coarse.1 = (bf16[512,512]{1,0:T(8,128)(2,1)}, bf16[512,256]{1,0:T(8,128)(2,1)}, bf16[256,16,128]{2,1,0:T(8,128)(2,1)}) custom-call(s32[1]{0:T(128)} %bitcast.1.core_ref, bf16[256,512]{1,0:T(8,128)(2,1)} %coarse_in.1.c_ref, bf16[256,512]{1,0:T(8,128)(2,1)} %copy-done.12, bf16[256,512]{1,0:T(8,128)(2,1)} %ct_ref.3, bf16[256,512]{1,0:T(8,128)(2,1)} %copy-done.11, ...), custom_call_target="tpu_custom_call" | custom-call | tf_op jit(solution)/shard_map/coarse/pallas_call | solution.py:273
  55.5 0.0 copy-done
  55.5 0.0 copy-done.1
  55.5 0.0 copy-done.2
  55.5 0.0 copy-done.4
  55.5 0.0 copy-done.6
  55.5 0.0 copy-done.9
  55.5 0.0 copy-start.3
  55.5 1.2 %copy-done.3 = bf16[256,16,128]{2,1,0:T(8,128)(2,1)S(1)} copy-done((bf16[256,16,128]{2,1,0:T(8,128)(2,1)S(1)}, bf16[256,16,128]{2,1,0:T(8,128)(2,1)}, u32[]{:S(2)}) %copy-start.3) | copy-done | bytes 1048600
  56.8 0.0 copy-start.7
  56.8 1.0 copy-done.7
  57.8 0.0 copy-start.10
  57.8 0.9 copy-done.10
  58.8 52.2 %tail.1 = (bf16[256,512]{1,0:T(8,128)(2,1)S(1)}, bf16[256,256]{1,0:T(8,128)(2,1)S(1)}, bf16[256,512]{1,0:T(8,128)(2,1)S(1)}, bf16[512,1536]{1,0:T(8,128)(2,1)S(1)}, bf16[512,512]{1,0:T(8,128)(2,1)S(1)}) custom-call(f32[288,640]{1,0:T(8,128)S(1)} %copy-done, f32[32,640]{1,0:T(8,128)S(1)} %copy-done.9, bf16[256,512]{1,0:T(8,128)(2,1)S(1)} %copy-done.4, ...), custom_call_target="tpu_custom_call" | custom-call | tf_op jit(solution)/shard_map/tail/pallas_call | solution.py:517
  111.0 0.7 copy.20
  111.7 0.7 copy.21
  112.4 0.7 copy.22
  113.1 1.1 copy.23
  114.2 0.8 copy.24
Async XLA Ops:
  0.6 27.1 %copy-start.5 = (bf16[256,512]{1,0:T(8,128)(2,1)S(1)}, bf16[256,512]{1,0:T(8,128)(2,1)}, u32[]{:S(2)}) copy-start(bf16[256,512]{1,0:T(8,128)(2,1)} %ct_ref.3) | copy-start | bytes 786436
  21.5 7.7 %collective-permute-start = (f32[32,640]{1,0:T(8,128)S(1)}, f32[32,640]{1,0:T(8,128)S(1)}, u32[]{:S(2)}, u32[]{:S(2)}) collective-permute-start(f32[32,640]{1,0:T(8,128)S(1)} %slice.4), channel_id=1, source_target_pairs={{0,1},{1,2},{2,3},{3,4},{4,5},{5,6},{6,7},{7,8},{8,9},{9,10},{10,1... | collective-permute-start | bytes 245768 | tf_op jit(solution)/shard_map/ppermute | solution.py:555
  27.7 4.4 %collective-permute-start.2 = (bf16[256,512]{1,0:T(8,128)(2,1)S(1)}, bf16[256,512]{1,0:T(8,128)(2,1)S(1)}, u32[]{:S(2)}, u32[]{:S(2)}) collective-permute-start(bf16[256,512]{1,0:T(8,128)(2,1)S(1)} %copy-done.5), channel_id=1, source_target_pairs={{0,1},{1,0},{2,3},{3,2},{4,5},{5,4},{6,7},{7,6},{8,9},{9,8},{10,11... | collective-permute-start | bytes 786440 | tf_op jit(solution)/shard_map/ppermute | solution.py:552
  29.2 0.6 copy-start.8
  32.2 1.7 %collective-permute-start.1 = (bf16[256,512]{1,0:T(8,128)(2,1)}, bf16[256,512]{1,0:T(8,128)(2,1)S(1)}, u32[]{:S(2)}, u32[]{:S(2)}) collective-permute-start(bf16[256,512]{1,0:T(8,128)(2,1)} %coarse_in.1.c_ref), channel_id=1, source_target_pairs={{0,1},{1,0},{2,3},{3,2},{4,5},{5,4},{6,7},{7,6},{8,9},{9,8},{10,11... | collective-permute-start | bytes 786440 | tf_op jit(solution)/shard_map/ppermute | solution.py:563
  32.2 1.7 %copy-start.11 = (bf16[256,512]{1,0:T(8,128)(2,1)}, bf16[256,512]{1,0:T(8,128)(2,1)S(1)}, u32[]{:S(2)}) copy-start(bf16[256,512]{1,0:T(8,128)(2,1)S(1)} %collective-permute-done.2.ctf_ref) | copy-start | bytes 786436
  33.9 0.7 copy-start.12
  34.6 20.9 %copy-start = (f32[288,640]{1,0:T(8,128)S(1)}, f32[288,640]{1,0:T(8,128)}, u32[]{:S(2)}) copy-start(f32[288,640]{1,0:T(8,128)} %fine.1.ab_ref) | copy-start | bytes 2211844
  34.6 20.9 %copy-start.1 = (bf16[256,512]{1,0:T(8,128)(2,1)S(1)}, bf16[256,512]{1,0:T(8,128)(2,1)}, u32[]{:S(2)}) copy-start(bf16[256,512]{1,0:T(8,128)(2,1)} %coarse_in.1.c_ref) | copy-start | bytes 786436
  34.6 20.9 %copy-start.2 = (bf16[512,512]{1,0:T(8,128)(2,1)S(1)}, bf16[512,512]{1,0:T(8,128)(2,1)}, u32[]{:S(2)}) copy-start(bf16[512,512]{1,0:T(8,128)(2,1)} %ow_ref.5) | copy-start | bytes 1572868
  34.6 20.9 %copy-start.4 = (bf16[256,512]{1,0:T(8,128)(2,1)S(1)}, bf16[256,512]{1,0:T(8,128)(2,1)}, u32[]{:S(2)}) copy-start(bf16[256,512]{1,0:T(8,128)(2,1)} %pw_ref.3) | copy-start | bytes 786436
  34.6 20.9 %copy-start.6 = (bf16[256,512]{1,0:T(8,128)(2,1)S(1)}, bf16[256,512]{1,0:T(8,128)(2,1)}, u32[]{:S(2)}) copy-start(bf16[256,512]{1,0:T(8,128)(2,1)} %ct_ref.3) | copy-start | bytes 786436
  34.7 20.9 %copy-start.9 = (f32[32,640]{1,0:T(8,128)S(1)}, f32[32,640]{1,0:T(8,128)}, u32[]{:S(2)}) copy-start(f32[32,640]{1,0:T(8,128)} %copy-done.8) | copy-start | bytes 245764
  55.5 1.2 %copy-start.3 = (bf16[256,16,128]{2,1,0:T(8,128)(2,1)S(1)}, bf16[256,16,128]{2,1,0:T(8,128)(2,1)}, u32[]{:S(2)}) copy-start(bf16[256,16,128]{2,1,0:T(8,128)(2,1)} %get-tuple-element.10.big) | copy-start | bytes 3145732
  56.8 1.0 copy-start.7
  57.8 0.9 copy-start.10

commit v3 on v2

--- a/solution.py
+++ b/solution.py
@@ -54,6 +54,8 @@
 
 def fine_kernel(cnt_ref, off_ref, x_ref, w_ref, ow_ref, ab_ref, k_ref, qt_ref, va_ref, mt_ref):
     count = cnt_ref[0]
+    shift = (lax.axis_index("rep") * lax.axis_size("pts") + lax.axis_index("pts")) * 256
+    offset = off_ref[...] - shift
     x = x_ref[...]
     n = normalize(x.astype(F32)).astype(BF)
     k_ref[...] = mm(n, w_ref[:, 256:512]).astype(BF)
@@ -117,7 +119,7 @@
         lax.fori_loop(0, 16, safe_head, 0)
 
     table = jnp.where(
-        (lax.broadcasted_iota(jnp.int32, (288, 1024), 0) == off_ref[...]) & live, 1.0, 0.0
+        (lax.broadcasted_iota(jnp.int32, (288, 1024), 0) == offset) & live, 1.0, 0.0
     )
     total = jnp.sum(table, axis=1, keepdims=True)
     table = table.astype(BF)
@@ -139,38 +141,79 @@
             pltpu.VMEM((16, 32, 1024), BF),
             pltpu.VMEM((256, 1024), BF),
         ],
-        compiler_params=pltpu.CompilerParams(vmem_limit_bytes=56 * 1024 * 1024),
+        compiler_params=pltpu.CompilerParams(vmem_limit_bytes=24 * 1024 * 1024),
         name="fine",
     )(count, offset, x, w, ow)
 
 
-def pooled(ab_ref, arr_ref, first, last):
-    top = ab_ref[:32, first:last] + arr_ref[:, first:last]
-    return jnp.concatenate([top, ab_ref[32:256, first:last]], axis=0)
-
-
-def pooled_mean(ab_ref, arr_ref, pw_ref):
-    a = pooled(ab_ref, arr_ref, 0, 256)
-    count = jnp.maximum(pooled(ab_ref, arr_ref, 512, 640)[:, :1], 1.0)
-    return split_dot(a, pw_ref[...]) / count, count
-
-
 GA = 0.7978845608028654
 GB = 0.044715
 
 
-def coarse_in_kernel(ab_ref, arr_ref, pw_ref, c_ref):
-    u, _ = pooled_mean(ab_ref, arr_ref, pw_ref)
+def pooled_mean(ab_ref, pw_ref):
+    count = jnp.maximum(ab_ref[:, 512:513], 1.0)
+    return split_dot(ab_ref[:, :256], pw_ref[...]) / count, count
+
+
+def middle_kernel(
+    ab_ref, pw_ref, ct_ref, sum_ref, c_ref, cf_ref, ctf_ref, arrived, send, recv
+):
+    rep = lax.axis_index("rep")
+    pts = lax.axis_index("pts")
+    total = lax.axis_size("pts")
+    ahead = (rep, (pts + 1) % total)
+    behind = (rep, (pts + total - 1) % total)
+    partner = (rep, pts + 1 - 2 * (pts % 2))
+    barrier = pltpu.get_barrier_semaphore()
+    for peer in (ahead, behind, partner):
+        pl.semaphore_signal(barrier, inc=1, device_id=peer, device_id_type=MESH)
+    pl.semaphore_wait(barrier, 3)
+
+    def push(i, src, dst, peer):
+        copy = pltpu.make_async_remote_copy(
+            src_ref=src, dst_ref=dst, send_sem=send.at[i], recv_sem=recv.at[i],
+            device_id=peer, device_id_type=MESH,
+        )
+        copy.start()
+        return copy
+
+    moved = push(0, ab_ref.at[pl.ds(256, 32)], arrived, ahead)
+    cot = push(1, ct_ref, ctf_ref, partner)
+    sum_ref[32:] = ab_ref[32:256]
+    moved.wait()
+    sum_ref[:32] = ab_ref[:32] + arrived[...]
+    u, _ = pooled_mean(sum_ref, pw_ref)
     c_ref[...] = (0.5 * u * (1.0 + jnp.tanh(GA * (u + GB * u * u * u)))).astype(BF)
+    push(2, c_ref, cf_ref, partner).wait()
+    cot.wait()
+
+
+def middle_call(ab, pw, ct):
+    half = jax.ShapeDtypeStruct((256, 512), BF)
+    return pl.pallas_call(
+        middle_kernel,
+        out_shape=(jax.ShapeDtypeStruct((256, 640), F32), half, half, half),
+        in_specs=[VM] * 3,
+        out_specs=(VM,) * 4,
+        scratch_shapes=[
+            pltpu.VMEM((32, 640), F32),
+            pltpu.SemaphoreType.DMA((3,)),
+            pltpu.SemaphoreType.DMA((3,)),
+        ],
+        compiler_params=pltpu.CompilerParams(
+            collective_id=1, has_side_effects=True, vmem_limit_bytes=12 * 1024 * 1024
+        ),
+        name="middle",
+    )(ab, pw, ct)
 
 
 def coarse_kernel(
-    core_ref, c_ref, cf_ref, ct_ref, ctf_ref, w_ref, ow_ref,
+    c_ref, cf_ref, ct_ref, ctf_ref, w_ref, ow_ref,
     dn_ref, mix_ref, g_ref,
     n_ref, cot_ref, k_ref, v_ref, kt_ref, qt_ref, va_ref, dot_ref, ot_ref, dp_ref,
     p_ref, pb_ref, ds_ref,
 ):
-    core = core_ref[0]
+    core = lax.axis_index("pts") % 2
     lo = pl.multiple_of(core * 256, 256)
     n_ref[:256] = normalize(c_ref[...].astype(F32)).astype(BF)
     n_ref[256:] = normalize(cf_ref[...].astype(F32)).astype(BF)
@@ -269,7 +312,7 @@
         g_ref[192 + j * 16 : 208 + j * 16] = block.reshape(16, 16, 128)
 
 
-def coarse_call(core, c, cf, ct, ctf, w, ow):
+def coarse_call(c, cf, ct, ctf, w, ow):
     return pl.pallas_call(
         coarse_kernel,
         out_shape=(
@@ -277,7 +320,7 @@
             jax.ShapeDtypeStruct((512, 256), BF),
             jax.ShapeDtypeStruct((256, 16, 128), BF),
         ),
-        in_specs=[SM, VM, VM, VM, VM, VM, VM],
+        in_specs=[VM] * 6,
         out_specs=(VM, VM, VM),
         scratch_shapes=[
             pltpu.VMEM((512, 512), BF),
@@ -294,9 +337,9 @@
             pltpu.VMEM((2, 512, 512), BF),
             pltpu.VMEM((2, 512, 512), BF),
         ],
-        compiler_params=pltpu.CompilerParams(vmem_limit_bytes=56 * 1024 * 1024),
+        compiler_params=pltpu.CompilerParams(vmem_limit_bytes=28 * 1024 * 1024),
         name="coarse",
-    )(core, c, cf, ct, ctf, w, ow)
+    )(c, cf, ct, ctf, w, ow)
 
 
 def other_one(v):
@@ -308,9 +351,9 @@
 
 
 def tail_kernel(
-    ab_ref, arr_ref, pw_ref, c_ref, ct_ref, dn_ref, mix_ref, ow_ref, big,
-    out_ref, gof_ref, gp_ref, gq_ref, goc_ref,
-    dnf, mixf, small, sm, g, r1, s1, r2, ra, rb, ha, hb, ra2, rb2, z, rz, zf, fa, fb, full,
+    ab_ref, pw_ref, c_ref, ct_ref, dn_ref, mix_ref, ow_ref, big,
+    out_ref, full,
+    dnf, mixf, small, sm, g, r1, s1, r2, ra, rb, ha, hb, ra2, rb2, z, rz, zf, fa, fb,
     send, recv,
 ):
     rep = lax.axis_index("rep")
@@ -375,12 +418,12 @@
         first.append(push(big.at[quarter(base, p)], r1.at[k, 0], place(p)))
 
     c = c_ref[...].astype(F32)
-    u, count = pooled_mean(ab_ref, arr_ref, pw_ref)
+    u, count = pooled_mean(ab_ref, pw_ref)
     th = jnp.tanh(GA * (u + GB * u * u * u))
     slope = 0.5 * (1.0 + th) + 0.5 * u * (1.0 - th * th) * (GA * (1.0 + 3.0 * GB * u * u))
     r = lax.rsqrt(jnp.mean(c * c, axis=-1, keepdims=True) + EPS)
-    at = jnp.transpose(pooled(ab_ref, arr_ref, 0, 256)).astype(BF)
-    bt = jnp.transpose(pooled(ab_ref, arr_ref, 256, 512)).astype(BF)
+    at = jnp.transpose(ab_ref[:, :256]).astype(BF)
+    bt = jnp.transpose(ab_ref[:, 256:512]).astype(BF)
     wait(trade)
     dn = dn_ref[:256].astype(F32) + dnf[...].astype(F32)
     inner = jnp.mean(dn * c, axis=-1, keepdims=True)
@@ -493,6 +536,10 @@
         done.append(share(quarter(base, one(v)), partner))
         done.append(share(quarter(base, two(one(v))), partner))
     wait(done)
+
+
+def unpack_kernel(out_ref, full, copy_ref, gof_ref, gp_ref, gq_ref, goc_ref):
+    copy_ref[...] = out_ref[...]
     for c in range(2):
         for j in range(6):
             column = (j // 2) * 512 + c * 256 + (j % 2) * 128
@@ -518,52 +565,52 @@
         tail_kernel,
         out_shape=(
             jax.ShapeDtypeStruct((256, 512), BF),
+            jax.ShapeDtypeStruct((2, 320, 16, 128), BF),
+        ),
+        in_specs=[VM] * 8,
+        out_specs=(VM,) * 2,
+        scratch_shapes=[
+            pltpu.VMEM((256, 512), BF), pltpu.VMEM((256, 256), BF),
+            tiles(2, 48), tiles(48), tiles(64),
+            tiles(4, 2, 16), tiles(4, 16), tiles(4, 16), tiles(3, 8), tiles(3, 8),
+            tiles(4, 10), tiles(4, 10), tiles(3, 10), tiles(3, 10),
+            tiles(24), tiles(7, 3), tiles(24), tiles(4, 10), tiles(4, 10),
+            pltpu.SemaphoreType.DMA((96,)),
+            pltpu.SemaphoreType.DMA((96,)),
+        ],
+        compiler_params=pltpu.CompilerParams(
+            collective_id=0, has_side_effects=True, vmem_limit_bytes=20 * 1024 * 1024
+        ),
+        name="tail",
+    )(*operands)
+
+
+def unpack_call(out, full):
+    return pl.pallas_call(
+        unpack_kernel,
+        out_shape=(
+            jax.ShapeDtypeStruct((256, 512), BF),
             jax.ShapeDtypeStruct((256, 256), BF),
             jax.ShapeDtypeStruct((256, 512), BF),
             jax.ShapeDtypeStruct((512, 1536), BF),
             jax.ShapeDtypeStruct((512, 512), BF),
         ),
-        in_specs=[VM] * 9,
+        in_specs=[VM] * 2,
         out_specs=(VM,) * 5,
-        scratch_shapes=[
-            pltpu.VMEM((256, 512), BF), pltpu.VMEM((256, 256), BF),
-            tiles(2, 48), tiles(48), tiles(64),
-            tiles(4, 2, 16), tiles(4, 16), tiles(4, 16), tiles(3, 8), tiles(3, 8),
-            tiles(4, 10), tiles(4, 10), tiles(3, 10), tiles(3, 10),
-            tiles(24), tiles(7, 3), tiles(24), tiles(4, 10), tiles(4, 10), tiles(2, 320),
-            pltpu.SemaphoreType.DMA((96,)),
-            pltpu.SemaphoreType.DMA((96,)),
-        ],
-        compiler_params=pltpu.CompilerParams(
-            collective_id=0, has_side_effects=True, vmem_limit_bytes=40 * 1024 * 1024
-        ),
-        name="tail",
-    )(*operands)
+        compiler_params=pltpu.CompilerParams(vmem_limit_bytes=12 * 1024 * 1024),
+        name="unpack",
+    )(out, full)
 
 
 def local(
     fine_points, parent, patch_count, qkv_fine, out_fine, pool_weight, qkv_coarse, out_coarse,
     cotangent,
 ):
-    pts = lax.axis_index("pts")
-    position = lax.axis_index("rep") * lax.axis_size("pts") + pts
-    core = (pts % 2).reshape(1)
-    swap = [(i, i ^ 1) for i in range(32)]
-    far_cot = lax.ppermute(cotangent, "pts", swap)
-    offset = (parent - position * 256).reshape(1, 1024)
-    ab = fine_call(patch_count, offset, fine_points, qkv_fine, out_fine)
-    arrived = lax.ppermute(ab[256:], "pts", [(i, i + 1) for i in range(31)])
-    coarse_in = pl.pallas_call(
-        coarse_in_kernel,
-        out_shape=jax.ShapeDtypeStruct((256, 512), BF),
-        in_specs=[VM, VM, VM],
-        out_specs=VM,
-        name="coarse_in",
-    )(ab, arrived, pool_weight)
-    far_in = lax.ppermute(coarse_in, "pts", swap)
-    dn, mixed, big = coarse_call(core, coarse_in, far_in, cotangent, far_cot, qkv_coarse, out_coarse)
-    return tail_call(
-        ab, arrived, pool_weight, coarse_in, cotangent, dn, mixed, out_coarse, big
+    ab = fine_call(patch_count, parent.reshape(1, 1024), fine_points, qkv_fine, out_fine)
+    sums, coarse_in, far_in, far_cot = middle_call(ab, pool_weight, cotangent)
+    dn, mixed, big = coarse_call(coarse_in, far_in, cotangent, far_cot, qkv_coarse, out_coarse)
+    return unpack_call(
+        *tail_call(sums, pool_weight, coarse_in, cotangent, dn, mixed, out_coarse, big)
     )
 
 

time: 115 us -> 101 us (0.88)
  starting transfers between devices: 6.35 us -> 0 us
  local copies, waits for them, and re-layouts: 9.47 us -> 3.64 us
  waiting for transfers between devices: 3.09 us -> 0 us
  Pallas kernels: 93.4 us -> 95.8 us
  other arithmetic: 1.28 us -> 0 us
    pallas_call x1 -> x2, Pallas kernels: 2.35 us -> 16.2 us  [the longest x1 14.3 us: middle_call(): pl.pallas_call(middle_kernel, out_shape=(jax.ShapeDtypeStruct((256, 640),...]
    ppermute x3 -> x0, starting transfers between devices: 6.35 us -> none  [the longest x1 6.26 us: local(): arrived = lax.ppermute(ab[256:], 'pts', [(i, i + 1) for i in range(31)])]
    pallas_call x1, Pallas kernels: 52.2 us -> 46.1 us  [tail_call(): pl.pallas_call(tail_kernel, out_shape=(jax.ShapeDtypeStruct((256, 512), B...]
    unnamed x31 -> x16, local copies, waits for them, and re-layouts: 8.58 us -> 3.64 us
    pallas_call x1, Pallas kernels: 20.8 us -> 17.6 us  [coarse_call(): pl.pallas_call(coarse_kernel, out_shape=(jax.ShapeDtypeStruct((512, 512),...]
    ppermute x3 -> x0, waiting for transfers between devices: 3.09 us -> none  [the longest x1 1.73 us: local(): far_in = lax.ppermute(coarse_in, 'pts', swap)]
    pallas_call x1, Pallas kernels: 17.9 us -> 15.8 us  [fine_call(): pl.pallas_call(fine_kernel, out_shape=jax.ShapeDtypeStruct((288, 640), F3...]
    sub x1 -> x0, other arithmetic: 1.28 us -> none  [local(): offset = (parent - position * 256).reshape(1, 1024)]
  transfers between devices with their start and end apart: 3 -> 0, of which waited for: 2 -> 0; matrix products, arithmetic and copies ran while one was open for 0% -> 0% of each run, Pallas kernels for 2% -> 0%
where the time goes in v3:
time: 101 us
  Pallas kernels  95.8 us (95%)
  local copies, waits for them, and re-layouts  3.64 us (4%)
  between operations  1.53 us (2%)
    pallas_call x1, Pallas kernels, tail_call(): pl.pallas_call(tail_kernel, out_shape=(jax.ShapeDtypeStruct((256, 512), B...  46.1 us
    pallas_call x1, Pallas kernels, coarse_call(): pl.pallas_call(coarse_kernel, out_shape=(jax.ShapeDtypeStruct((512, 512),...  17.6 us
    pallas_call x1, Pallas kernels, fine_call(): pl.pallas_call(fine_kernel, out_shape=jax.ShapeDtypeStruct((288, 640), F3...  15.8 us
    pallas_call x1, Pallas kernels, middle_call(): pl.pallas_call(middle_kernel, out_shape=(jax.ShapeDtypeStruct((256, 640),...  14.3 us
    unnamed x16, local copies, waits for them, and re-layouts  3.64 us

profile of v3, /device:TPU:1, one launch (start us, length us, event | category | flops | bytes accessed | tf_op | source)
XLA Modules:
  0.0 101.0 jit_solution(1204951476654101793)
XLA Ops:
  0.6 0.0 copy-start
  0.6 0.0 copy-start.1
  0.7 0.0 copy-start.3
  0.7 0.0 copy-start.2
  1.5 0.0 copy-start.4
  1.5 1.0 %copy-done.4 = bf16[1024,256]{1,0:T(8,128)(2,1)S(1)} copy-done((bf16[1024,256]{1,0:T(8,128)(2,1)S(1)}, bf16[1024,256]{1,0:T(8,128)(2,1)}, u32[]{:S(2)}) %copy-start.4) | copy-done | bytes 524312
  2.5 0.0 copy-start.5
  2.5 1.0 copy-done.5
  3.5 0.0 copy-start.6
  3.5 0.9 copy-done.6
  4.4 0.0 copy-start.7
  4.4 0.7 copy-done.7
  5.1 15.8 %fine.1.ab_ref = f32[288,640]{1,0:T(8,128)S(1)} custom-call(s32[1]{0:T(128)S(6)} %copy.14.cnt_ref, s32[1,1024]{1,0:T(1,128)S(1)} %bitcast.1, bf16[1024,256]{1,0:T(8,128)(2,1)S(1)} %copy-done.4, bf16[256,768]{1,0:T(8,128)(2,1)S(1)} %copy-done.5, bf16[256,256]{1,0:T(8,128)(2,1)S(1)} %copy-done.6), custom_call_target="tpu_custom_call" | custom-call | tf_op jit(solution)/shard_map/fine/pallas_call | solution.py:133
  20.9 0.0 copy-done
  21.0 0.0 copy-done.3
  21.0 14.3 %middle.1 = (f32[256,640]{1,0:T(8,128)S(1)}, bf16[256,512]{1,0:T(8,128)(2,1)S(1)}, bf16[256,512]{1,0:T(8,128)(2,1)S(1)}, bf16[256,512]{1,0:T(8,128)(2,1)S(1)}) custom-call(f32[288,640]{1,0:T(8,128)S(1)} %fine.1.ab_ref, bf16[256,512]{1,0:T(8,128)(2,1)S(1)} %copy-done.3, bf16[256,512]{1,0:T(8,128)(2,1)S(1)} %copy-done), custom_call_target="tpu_custom_call" | custom-call | tf_op jit(solution)/shard_map/middle/pallas_call | solution.py:193
  35.2 0.0 copy-done.1
  35.3 0.0 copy-done.2
  35.3 17.6 %coarse.1 = (bf16[512,512]{1,0:T(8,128)(2,1)S(1)}, bf16[512,256]{1,0:T(8,128)(2,1)S(1)}, bf16[256,16,128]{2,1,0:T(8,128)(2,1)S(1)}) custom-call(bf16[256,512]{1,0:T(8,128)(2,1)S(1)} %get-tuple-element.15.c_ref, bf16[256,512]{1,0:T(8,128)(2,1)S(1)} %get-tuple-element.16.cf_ref, bf16[256,512]{1,0:T(8,128)(2,1)S(1)} %copy-done, ...), custom_call_target="tpu_custom_call" | custom-call | tf_op jit(solution)/shard_map/coarse/pallas_call | solution.py:316
  52.9 46.1 %tail.1 = (bf16[256,512]{1,0:T(8,128)(2,1)S(1)}, bf16[2,320,16,128]{3,2,1,0:T(8,128)(2,1)S(1)}) custom-call(f32[256,640]{1,0:T(8,128)S(1)} %get-tuple-element.14.ab_ref, bf16[256,512]{1,0:T(8,128)(2,1)S(1)} %copy-done.3, bf16[256,512]{1,0:T(8,128)(2,1)S(1)} %get-tuple-element.15.c_ref, bf16[256,512]{1,0:T(8,128)(2,1)S(1)} %copy-done, ...), custom_call_target="tpu_custom_call" | custom-call | tf_op jit(solution)/shard_map/tail/pallas_call | solution.py:564
  99.0 2.0 %unpack.1 = (bf16[256,512]{1,0:T(8,128)(2,1)}, bf16[256,256]{1,0:T(8,128)(2,1)}, bf16[256,512]{1,0:T(8,128)(2,1)}, bf16[512,1536]{1,0:T(8,128)(2,1)}, bf16[512,512]{1,0:T(8,128)(2,1)}) custom-call(bf16[256,512]{1,0:T(8,128)(2,1)S(1)} %get-tuple-element.21.out_ref, bf16[2,320,16,128]{3,2,1,0:T(8,128)(2,1)S(1)} %get-tuple-element.22.full), custom_call_target="tpu_custom_call" | custom-call | tf_op jit(solution)/shard_map/unpack/pallas_call | solution.py:589
Async XLA Ops:
  0.6 20.3 %copy-start = (bf16[256,512]{1,0:T(8,128)(2,1)S(1)}, bf16[256,512]{1,0:T(8,128)(2,1)}, u32[]{:S(2)}) copy-start(bf16[256,512]{1,0:T(8,128)(2,1)} %ct_ref.5) | copy-start | bytes 786436
  0.6 34.6 %copy-start.1 = (bf16[512,512]{1,0:T(8,128)(2,1)S(1)}, bf16[512,512]{1,0:T(8,128)(2,1)}, u32[]{:S(2)}) copy-start(bf16[512,512]{1,0:T(8,128)(2,1)} %ow_ref.5) | copy-start | bytes 1572868
  0.7 20.3 %copy-start.3 = (bf16[256,512]{1,0:T(8,128)(2,1)S(1)}, bf16[256,512]{1,0:T(8,128)(2,1)}, u32[]{:S(2)}) copy-start(bf16[256,512]{1,0:T(8,128)(2,1)} %pw_ref.3) | copy-start | bytes 786436
  0.7 34.6 %copy-start.2 = (bf16[512,1536]{1,0:T(8,128)(2,1)S(1)}, bf16[512,1536]{1,0:T(8,128)(2,1)}, u32[]{:S(2)}) copy-start(bf16[512,1536]{1,0:T(8,128)(2,1)} %w_ref.3) | copy-start | bytes 4718596
  1.5 1.0 %copy-start.4 = (bf16[1024,256]{1,0:T(8,128)(2,1)S(1)}, bf16[1024,256]{1,0:T(8,128)(2,1)}, u32[]{:S(2)}) copy-start(bf16[1024,256]{1,0:T(8,128)(2,1)} %x_ref.1) | copy-start | bytes 1572868
  2.5 1.0 copy-start.5
  3.5 0.9 copy-start.6
  4.4 0.7 copy-start.7

commit v4 on v3

--- a/solution.py
+++ b/solution.py
@@ -52,12 +52,23 @@
     return jnp.max(q2) * jnp.max(k2)
 
 
-def fine_kernel(cnt_ref, off_ref, x_ref, w_ref, ow_ref, ab_ref, k_ref, qt_ref, va_ref, mt_ref):
+def fine_kernel(
+    cnt_ref, off_hbm, x_hbm, w_hbm, ow_hbm, ab_ref,
+    k_ref, qt_ref, va_ref, mt_ref, off_ref, x_ref, w_ref, ow_ref, load,
+):
+    pairs = ((x_hbm, x_ref), (w_hbm, w_ref), (off_hbm, off_ref), (ow_hbm, ow_ref))
+    loads = [pltpu.make_async_copy(a, b, load.at[i]) for i, (a, b) in enumerate(pairs)]
+    for copy in loads:
+        copy.start()
     count = cnt_ref[0]
     shift = (lax.axis_index("rep") * lax.axis_size("pts") + lax.axis_index("pts")) * 256
-    offset = off_ref[...] - shift
+    loads[0].wait()
     x = x_ref[...]
     n = normalize(x.astype(F32)).astype(BF)
+    loads[1].wait()
+    loads[2].wait()
+    loads[3].wait()
+    offset = off_ref[...] - shift
     k_ref[...] = mm(n, w_ref[:, 256:512]).astype(BF)
     qt_ref[...] = (mm(w_ref[:, :256], n, TT) * (0.25 * LOG2E)).astype(BF)
     vt = mm(w_ref[:, 512:], n, TT).astype(BF)
@@ -133,13 +144,18 @@
     return pl.pallas_call(
         fine_kernel,
         out_shape=jax.ShapeDtypeStruct((288, 640), F32),
-        in_specs=[SM, VM, VM, VM, VM],
+        in_specs=[SM] + [pl.BlockSpec(memory_space=pltpu.HBM)] * 4,
         out_specs=VM,
         scratch_shapes=[
             pltpu.VMEM((1024, 256), BF),
             pltpu.VMEM((256, 1024), BF),
             pltpu.VMEM((16, 32, 1024), BF),
             pltpu.VMEM((256, 1024), BF),
+            pltpu.VMEM((1, 1024), jnp.int32),
+            pltpu.VMEM((1024, 256), BF),
+            pltpu.VMEM((256, 768), BF),
+            pltpu.VMEM((256, 256), BF),
+            pltpu.SemaphoreType.DMA((4,)),
         ],
         compiler_params=pltpu.CompilerParams(vmem_limit_bytes=24 * 1024 * 1024),
         name="fine",
@@ -150,9 +166,13 @@
 GB = 0.044715
 
 
-def pooled_mean(ab_ref, pw_ref):
-    count = jnp.maximum(ab_ref[:, 512:513], 1.0)
-    return split_dot(ab_ref[:, :256], pw_ref[...]) / count, count
+def pooled_mean(sums, pw_ref):
+    count = jnp.maximum(sums[:, 512:513], 1.0)
+    return split_dot(sums[:, :256], pw_ref[...]) / count, count
+
+
+def gelu(u):
+    return 0.5 * u * (1.0 + jnp.tanh(GA * (u + GB * u * u * u)))
 
 
 def middle_kernel(
@@ -167,6 +187,9 @@
     barrier = pltpu.get_barrier_semaphore()
     for peer in (ahead, behind, partner):
         pl.semaphore_signal(barrier, inc=1, device_id=peer, device_id_type=MESH)
+    own, _ = pooled_mean(ab_ref[32:256], pw_ref)
+    sum_ref[32:] = ab_ref[32:256]
+    c_ref[32:] = gelu(own).astype(BF)
     pl.semaphore_wait(barrier, 3)
 
     def push(i, src, dst, peer):
@@ -179,13 +202,16 @@
 
     moved = push(0, ab_ref.at[pl.ds(256, 32)], arrived, ahead)
     cot = push(1, ct_ref, ctf_ref, partner)
-    sum_ref[32:] = ab_ref[32:256]
+    rest = push(2, c_ref.at[pl.ds(32, 224)], cf_ref.at[pl.ds(32, 224)], partner)
     moved.wait()
-    sum_ref[:32] = ab_ref[:32] + arrived[...]
-    u, _ = pooled_mean(sum_ref, pw_ref)
-    c_ref[...] = (0.5 * u * (1.0 + jnp.tanh(GA * (u + GB * u * u * u)))).astype(BF)
-    push(2, c_ref, cf_ref, partner).wait()
+    first = ab_ref[:32] + arrived[...]
+    sum_ref[:32] = first
+    u, _ = pooled_mean(first, pw_ref)
+    c_ref[:32] = gelu(u).astype(BF)
+    last = push(3, c_ref.at[pl.ds(0, 32)], cf_ref.at[pl.ds(0, 32)], partner)
     cot.wait()
+    rest.wait()
+    last.wait()
 
 
 def middle_call(ab, pw, ct):
@@ -197,8 +223,8 @@
         out_specs=(VM,) * 4,
         scratch_shapes=[
             pltpu.VMEM((32, 640), F32),
-            pltpu.SemaphoreType.DMA((3,)),
-            pltpu.SemaphoreType.DMA((3,)),
+            pltpu.SemaphoreType.DMA((4,)),
+            pltpu.SemaphoreType.DMA((4,)),
         ],
         compiler_params=pltpu.CompilerParams(
             collective_id=1, has_side_effects=True, vmem_limit_bytes=12 * 1024 * 1024
@@ -353,8 +379,8 @@
 def tail_kernel(
     ab_ref, pw_ref, c_ref, ct_ref, dn_ref, mix_ref, ow_ref, big,
     out_ref, full,
-    dnf, mixf, small, sm, g, r1, s1, r2, ra, rb, ha, hb, ra2, rb2, z, rz, zf, fa, fb,
-    send, recv,
+    dnf, mixf, slope_ref, at_ref, bt_ref, small, sm, g, r1, s1, r2, ra, rb,
+    ha, hb, ra2, rb2, z, rz, zf, fa, fb, send, recv,
 ):
     rep = lax.axis_index("rep")
     pts = lax.axis_index("pts")
@@ -381,6 +407,14 @@
     peers += [at_z((zi + d) % 8) for d in range(1, 8)]
     for peer in peers:
         pl.semaphore_signal(barrier, inc=1, device_id=peer, device_id_type=MESH)
+    c = c_ref[...].astype(F32)
+    u, count = pooled_mean(ab_ref[...], pw_ref)
+    th = jnp.tanh(GA * (u + GB * u * u * u))
+    slope = 0.5 * (1.0 + th) + 0.5 * u * (1.0 - th * th) * (GA * (1.0 + 3.0 * GB * u * u))
+    slope_ref[...] = slope / count
+    r = lax.rsqrt(jnp.mean(c * c, axis=-1, keepdims=True) + EPS)
+    at_ref[...] = jnp.transpose(ab_ref[:, :256]).astype(BF)
+    bt_ref[...] = jnp.transpose(ab_ref[:, 256:512]).astype(BF)
     pl.semaphore_wait(barrier, len(peers))
 
     counter = [0]
@@ -395,146 +429,168 @@
         copy.start()
         return copy
 
+    def share(rows, peer):
+        spot = full.at[core, rows]
+        return push(spot, spot, peer)
+
     def wait(copies):
         for copy in copies:
             copy.wait()
 
-    streams = [
-        (x, at_x, 0, other_one, other_two),
-        (x, at_x, 64, other_two, other_one),
-        (y, at_y, 128, other_one, other_two),
-        (y, at_y, 192, other_two, other_one),
-    ]
+    def f32(value):
+        return value.astype(F32)
+
+    def add(own, slots):
+        total = f32(own)
+        for slot in slots:
+            total = total + f32(slot)
+        return total.astype(BF)
 
     def quarter(base, v):
-        return pl.ds(base + v * 16, 16)
+        return pl.ds(base + v * 8, 8)
+
+    third, done = [], []
+
+    def chain(m):
+        streams = [
+            (x, at_x, m * 128, other_one, other_two),
+            (x, at_x, m * 128 + 32, other_two, other_one),
+            (y, at_y, m * 128 + 64, other_one, other_two),
+            (y, at_y, m * 128 + 96, other_two, other_one),
+        ]
+        n = 4 + 2 * m
+        w = 1 + m
+        some = pl.ds(0, n)
+        few = pl.ds(0, w)
+        first = []
+        for k, (v, place, base, one, two) in enumerate(streams):
+            p = one(v)
+            first.append(push(big.at[quarter(base, two(p))], r1.at[m, k, 1], place(p)))
+            first.append(push(big.at[quarter(base, p)], r1.at[m, k, 0], place(p)))
+        yield
+        second = []
+        for k, (v, place, base, one, two) in enumerate(streams):
+            wait(first[2 * k : 2 * k + 2])
+            s1[m, k] = add(big[quarter(base, two(v))], [r1[m, k, 1]])
+            second.append(push(s1.at[m, k], r2.at[m, k], place(two(v))))
+        yield
+        for k, (v, place, base, one, two) in enumerate(streams):
+            second[k].wait()
+            total = add(big[quarter(base, v)], [r1[m, k, 0], r2[m, k]])
+            keep = ha if k < 2 else hb
+            spot = (k % 2) * 2
+            keep[m, :, spot : spot + 2] = total.reshape(4, 2, 16, 128)
+        if m:
+            wait(third)
+            total = add(g[pl.ds(x * 8, 8)], [ra[d] for d in range(3)])
+            ha[m, :, 4:] = total.reshape(4, 2, 16, 128)
+            total = add(g[pl.ds(32 + y * 8, 8)], [rb[d] for d in range(3)])
+            hb[m, :, 4:] = total.reshape(4, 2, 16, 128)
+        moves = []
+        for d in (2, 1, 3):
+            to = (y + d) % 4
+            moves.append(push(ha.at[m, to, some], ra2.at[m, d - 1, some], at_y(to)))
+            to = (x + d) % 4
+            moves.append(push(hb.at[m, to, some], rb2.at[m, d - 1, some], at_x(to)))
+        yield
+        wait(moves)
+        z[m, :n] = add(ha[m, y, :n], [ra2[m, d, :n] for d in range(3)])
+        z[m, n : 2 * n] = add(hb[m, x, :n], [rb2[m, d, :n] for d in range(3)])
+        if m:
+            z[m, 12:] = jnp.zeros((4, 16, 128), BF)
+        moves = []
+        for d in (4, 3, 5, 2, 6, 1, 7):
+            to = (zi + d) % 8
+            moves.append(push(z.at[m, pl.ds(to * w, w)], rz.at[m, d - 1, few], at_z(to)))
+        yield
+        wait(moves)
+        mine = pl.ds(zi * w, w)
+        zf[m, mine] = add(z[m, mine], [rz[m, d, :w] for d in range(7)])
+        spot = zf.at[m, mine]
+        moves = [push(spot, spot, at_z((zi + d) % 8)) for d in (4, 3, 5, 2, 6, 1, 7)]
+        yield
+        wait(moves)
+        fa[m, y, :n] = zf[m, :n]
+        fb[m, x, :n] = zf[m, n : 2 * n]
+        moves = []
+        for d in (2, 1, 3):
+            spot = fa.at[m, y, some]
+            moves.append(push(spot, spot, at_y((y + d) % 4)))
+            spot = fb.at[m, x, some]
+            moves.append(push(spot, spot, at_x((x + d) % 4)))
+        yield
+        wait(moves)
+        first, second, ups = [], [], []
+        for k, (v, place, base, one, two) in enumerate(streams):
+            kept = fa if k < 2 else fb
+            spot = (k % 2) * 2
+            own = quarter(base, v)
+            full[core, own] = kept[m, :, spot : spot + 2].reshape(8, 16, 128)
+            first.append(share(own, place(two(v))))
+            second.append(share(own, place(one(v))))
+            done.append(share(own, partner))
+        if m:
+            la, lb = pl.ds(256 + x * 8, 8), pl.ds(288 + y * 8, 8)
+            full[core, la] = fa[m, :, 4:].reshape(8, 16, 128)
+            full[core, lb] = fb[m, :, 4:].reshape(8, 16, 128)
+            for d in (2, 1, 3):
+                ups.append(share(la, at_x((x + d) % 4)))
+                ups.append(share(lb, at_y((y + d) % 4)))
+        yield
+        for k, (v, place, base, one, two) in enumerate(streams):
+            first[k].wait()
+            came = quarter(base, two(v))
+            second.append(share(came, place(one(v))))
+            done.append(share(came, partner))
+        yield
+        if m:
+            wait(ups)
+            done.append(share(pl.ds(256, 48), partner))
+        for k, (v, place, base, one, two) in enumerate(streams):
+            second[k].wait()
+            second[4 + k].wait()
+            done.append(share(quarter(base, one(v)), partner))
+            done.append(share(quarter(base, two(one(v))), partner))
 
     trade = [push(dn_ref.at[pl.ds(256, 256)], dnf, partner)]
     trade.append(push(mix_ref.at[pl.ds(256, 256)], mixf, partner))
-    first = []
-    for k, (v, place, base, one, two) in enumerate(streams):
-        p = one(v)
-        first.append(push(big.at[quarter(base, two(p))], r1.at[k, 1], place(p)))
-        first.append(push(big.at[quarter(base, p)], r1.at[k, 0], place(p)))
-
-    c = c_ref[...].astype(F32)
-    u, count = pooled_mean(ab_ref, pw_ref)
-    th = jnp.tanh(GA * (u + GB * u * u * u))
-    slope = 0.5 * (1.0 + th) + 0.5 * u * (1.0 - th * th) * (GA * (1.0 + 3.0 * GB * u * u))
-    r = lax.rsqrt(jnp.mean(c * c, axis=-1, keepdims=True) + EPS)
-    at = jnp.transpose(ab_ref[:, :256]).astype(BF)
-    bt = jnp.transpose(ab_ref[:, 256:512]).astype(BF)
+    halves = [chain(0), chain(1)]
+    next(halves[0])
+    next(halves[1])
     wait(trade)
-    dn = dn_ref[:256].astype(F32) + dnf[...].astype(F32)
+    dn = f32(dn_ref[:256]) + f32(dnf[...])
     inner = jnp.mean(dn * c, axis=-1, keepdims=True)
-    dc = r * dn - c * (r * r * r * inner) + ct_ref[...].astype(F32)
-    gs = (slope * dc / count).astype(BF)
+    dc = r * dn - c * (r * r * r * inner) + f32(ct_ref[...])
+    gs = (slope_ref[...] * dc).astype(BF)
     gw = mm(gs, pw_ref[...], NT).astype(BF)
     for half in range(2):
         rows = slice(half * 128, half * 128 + 128)
         for j in range(4):
-            block = mm(at[rows], gs[:, j * 128 : j * 128 + 128]).astype(BF)
+            block = mm(at_ref[rows], gs[:, j * 128 : j * 128 + 128]).astype(BF)
             small[half, j * 8 : j * 8 + 8] = block.reshape(8, 16, 128)
         for j in range(2):
-            block = mm(bt[rows], gw[:, j * 128 : j * 128 + 128]).astype(BF)
+            block = mm(bt_ref[rows], gw[:, j * 128 : j * 128 + 128]).astype(BF)
             small[half, 32 + j * 8 : 40 + j * 8] = block.reshape(8, 16, 128)
     swap = push(small.at[1 - core], sm, partner)
-
-    def f32(value):
-        return value.astype(F32)
-
-    second = []
-    for k, (v, place, base, one, two) in enumerate(streams):
-        wait(first[2 * k : 2 * k + 2])
-        s1[k] = (f32(big[quarter(base, two(v))]) + f32(r1[k, 1])).astype(BF)
-        second.append(push(s1.at[k], r2.at[k], place(two(v))))
+    next(halves[0])
     swap.wait()
-    g[:48] = (f32(small[core]) + f32(sm[...])).astype(BF)
+    g[:48] = add(small[core], [sm[...]])
     g[48:] = jnp.zeros((16, 16, 128), BF)
-    third = []
-    for d in (1, 2, 3):
+    next(halves[1])
+    for d in (2, 1, 3):
         to = (x + d) % 4
         third.append(push(g.at[pl.ds(to * 8, 8)], ra.at[d - 1], at_x(to)))
         to = (y + d) % 4
         third.append(push(g.at[pl.ds(32 + to * 8, 8)], rb.at[d - 1], at_y(to)))
+    next(halves[0])
     lo = pl.multiple_of(core * 256, 256)
     hi = pl.multiple_of(256 - core * 256, 256)
     mixed = mm(mix_ref[:256], ow_ref[pl.ds(lo, 256), :]) + mm(mixf[...], ow_ref[pl.ds(hi, 256), :])
-    out_ref[...] = (c + mixed).astype(BF)
-
-    def add(own, slots, n):
-        total = f32(own)
-        for d in range(n):
-            total = total + f32(slots[d])
-        return total.astype(BF)
-
-    for k, (v, place, base, one, two) in enumerate(streams):
-        second[k].wait()
-        total = (f32(big[quarter(base, v)]) + f32(r1[k, 0]) + f32(r2[k])).astype(BF)
-        keep = ha if k < 2 else hb
-        spot = (k % 2) * 4
-        keep[:, spot : spot + 4] = total.reshape(4, 4, 16, 128)
-    wait(third)
-    ha[:, 8:] = add(g[pl.ds(x * 8, 8)], ra, 3).reshape(4, 2, 16, 128)
-    hb[:, 8:] = add(g[pl.ds(32 + y * 8, 8)], rb, 3).reshape(4, 2, 16, 128)
-    moves = []
-    for d in (1, 2, 3):
-        to = (y + d) % 4
-        moves.append(push(ha.at[to], ra2.at[d - 1], at_y(to)))
-        to = (x + d) % 4
-        moves.append(push(hb.at[to], rb2.at[d - 1], at_x(to)))
-    wait(moves)
-    z[:10] = add(ha[y], ra2, 3)
-    z[10:20] = add(hb[x], rb2, 3)
-    z[20:] = jnp.zeros((4, 16, 128), BF)
-    moves = []
-    for d in (4, 3, 5, 2, 6, 1, 7):
-        to = (zi + d) % 8
-        moves.append(push(z.at[pl.ds(to * 3, 3)], rz.at[d - 1], at_z(to)))
-    wait(moves)
-    mine = pl.ds(zi * 3, 3)
-    zf[mine] = add(z[mine], rz, 7)
-    wait([push(zf.at[mine], zf.at[mine], at_z((zi + d) % 8)) for d in (4, 3, 5, 2, 6, 1, 7)])
-    fa[y] = zf[:10]
-    fb[x] = zf[10:20]
-    moves = []
-    for d in (1, 2, 3):
-        moves.append(push(fa.at[y], fa.at[y], at_y((y + d) % 4)))
-        moves.append(push(fb.at[x], fb.at[x], at_x((x + d) % 4)))
-    wait(moves)
-
-    def share(rows, peer):
-        spot = full.at[core, rows]
-        return push(spot, spot, peer)
-
-    ups = []
-    first, second, done = [], [], []
-    for k, (v, place, base, one, two) in enumerate(streams):
-        kept = fa if k < 2 else fb
-        spot = (k % 2) * 4
-        own = quarter(base, v)
-        full[core, own] = kept[:, spot : spot + 4].reshape(16, 16, 128)
-        first.append(share(own, place(two(v))))
-        second.append(share(own, place(one(v))))
-        done.append(share(own, partner))
-    la, lb = pl.ds(256 + x * 8, 8), pl.ds(288 + y * 8, 8)
-    full[core, la] = fa[:, 8:].reshape(8, 16, 128)
-    full[core, lb] = fb[:, 8:].reshape(8, 16, 128)
-    for d in (1, 2, 3):
-        ups.append(share(la, at_x((x + d) % 4)))
-        ups.append(share(lb, at_y((y + d) % 4)))
-    for k, (v, place, base, one, two) in enumerate(streams):
-        first[k].wait()
-        came = quarter(base, two(v))
-        second.append(share(came, place(one(v))))
-        done.append(share(came, partner))
-    wait(ups)
-    done.append(share(pl.ds(256, 48), partner))
-    for k, (v, place, base, one, two) in enumerate(streams):
-        second[k].wait()
-        second[4 + k].wait()
-        done.append(share(quarter(base, one(v)), partner))
-        done.append(share(quarter(base, two(one(v))), partner))
+    out_ref[...] = (f32(c_ref[...]) + mixed).astype(BF)
+    next(halves[1])
+    for _ in range(7):
+        for half in halves:
+            next(half, None)
     wait(done)
 
 
@@ -571,12 +627,13 @@
         out_specs=(VM,) * 2,
         scratch_shapes=[
             pltpu.VMEM((256, 512), BF), pltpu.VMEM((256, 256), BF),
+            pltpu.VMEM((256, 512), F32), pltpu.VMEM((256, 256), BF), pltpu.VMEM((256, 256), BF),
             tiles(2, 48), tiles(48), tiles(64),
-            tiles(4, 2, 16), tiles(4, 16), tiles(4, 16), tiles(3, 8), tiles(3, 8),
-            tiles(4, 10), tiles(4, 10), tiles(3, 10), tiles(3, 10),
-            tiles(24), tiles(7, 3), tiles(24), tiles(4, 10), tiles(4, 10),
-            pltpu.SemaphoreType.DMA((96,)),
-            pltpu.SemaphoreType.DMA((96,)),
+            tiles(2, 4, 2, 8), tiles(2, 4, 8), tiles(2, 4, 8), tiles(3, 8), tiles(3, 8),
+            tiles(2, 4, 6), tiles(2, 4, 6), tiles(2, 3, 6), tiles(2, 3, 6),
+            tiles(2, 16), tiles(2, 7, 2), tiles(2, 16), tiles(2, 4, 6), tiles(2, 4, 6),
+            pltpu.SemaphoreType.DMA((150,)),
+            pltpu.SemaphoreType.DMA((150,)),
         ],
         compiler_params=pltpu.CompilerParams(
             collective_id=0, has_side_effects=True, vmem_limit_bytes=20 * 1024 * 1024

time: 101 us -> 98.9 us (0.979)
  Pallas kernels: 95.8 us -> 93.5 us
    pallas_call x1, Pallas kernels: 46.1 us -> 43.7 us  [tail_call(): pl.pallas_call(tail_kernel, out_shape=(jax.ShapeDtypeStruct((256, 512), B...]
where the time goes in v4:
time: 98.9 us; the launch traced here: 98.7 us
  Pallas kernels  93.5 us (95%)
  local copies, waits for them, and re-layouts  3.64 us (4%)
  between operations  1.53 us (2%)
    pallas_call x1, Pallas kernels, tail_call(): pl.pallas_call(tail_kernel, out_shape=(jax.ShapeDtypeStruct((256, 512), B...  43.7 us
    pallas_call x1, Pallas kernels, coarse_call(): pl.pallas_call(coarse_kernel, out_shape=(jax.ShapeDtypeStruct((512, 512),...  17.6 us
    pallas_call x1, Pallas kernels, fine_call(): pl.pallas_call(fine_kernel, out_shape=jax.ShapeDtypeStruct((288, 640), F3...  16.4 us
    pallas_call x1, Pallas kernels, middle_call(): pl.pallas_call(middle_kernel, out_shape=(jax.ShapeDtypeStruct((256, 640),...  13.7 us
    unnamed x16, local copies, waits for them, and re-layouts  3.64 us

profile of v4, /device:TPU:1, one launch (start us, length us, event | category | flops | bytes accessed | tf_op | source)
XLA Modules:
  0.0 98.7 jit_solution(11773367304429480673)
XLA Ops:
  0.6 0.0 copy-start
  0.6 0.0 copy-start.1
  0.7 0.0 copy-start.3
  0.7 0.0 copy-start.2
  1.5 0.0 copy-start.4
  1.5 1.0 %copy-done.4 = bf16[1024,256]{1,0:T(8,128)(2,1)S(1)} copy-done((bf16[1024,256]{1,0:T(8,128)(2,1)S(1)}, bf16[1024,256]{1,0:T(8,128)(2,1)}, u32[]{:S(2)}) %copy-start.4) | copy-done | bytes 524312
  2.5 0.0 copy-start.5
  2.5 1.0 %copy-done.5 = bf16[256,768]{1,0:T(8,128)(2,1)S(1)} copy-done((bf16[256,768]{1,0:T(8,128)(2,1)S(1)}, bf16[256,768]{1,0:T(8,128)(2,1)}, u32[]{:S(2)}) %copy-start.5) | copy-done | bytes 393240
  3.5 0.0 copy-start.6
  3.5 0.9 copy-done.6
  4.4 0.0 copy-start.7
  4.4 0.7 copy-done.7
  5.1 16.4 %fine.1.ab_ref = f32[288,640]{1,0:T(8,128)S(1)} custom-call(s32[1]{0:T(128)S(6)} %copy.14.cnt_ref, s32[1,1024]{1,0:T(1,128)S(1)} %bitcast.1, bf16[1024,256]{1,0:T(8,128)(2,1)S(1)} %copy-done.4, bf16[256,768]{1,0:T(8,128)(2,1)S(1)} %copy-done.5, bf16[256,256]{1,0:T(8,128)(2,1)S(1)} %copy-done.6), custom_call_target="tpu_custom_call" | custom-call | tf_op jit(solution)/shard_map/fine/pallas_call | solution.py:144
  21.5 0.0 copy-done
  21.5 0.0 copy-done.3
  21.6 13.7 %middle.1 = (f32[256,640]{1,0:T(8,128)S(1)}, bf16[256,512]{1,0:T(8,128)(2,1)S(1)}, bf16[256,512]{1,0:T(8,128)(2,1)S(1)}, bf16[256,512]{1,0:T(8,128)(2,1)S(1)}) custom-call(f32[288,640]{1,0:T(8,128)S(1)} %fine.1.ab_ref, bf16[256,512]{1,0:T(8,128)(2,1)S(1)} %copy-done.3, bf16[256,512]{1,0:T(8,128)(2,1)S(1)} %copy-done), custom_call_target="tpu_custom_call" | custom-call | tf_op jit(solution)/shard_map/middle/pallas_call | solution.py:219
  35.3 0.0 copy-done.1
  35.3 0.0 copy-done.2
  35.3 17.6 %coarse.1 = (bf16[512,512]{1,0:T(8,128)(2,1)S(1)}, bf16[512,256]{1,0:T(8,128)(2,1)S(1)}, bf16[256,16,128]{2,1,0:T(8,128)(2,1)S(1)}) custom-call(bf16[256,512]{1,0:T(8,128)(2,1)S(1)} %get-tuple-element.15.c_ref, bf16[256,512]{1,0:T(8,128)(2,1)S(1)} %get-tuple-element.16.cf_ref, bf16[256,512]{1,0:T(8,128)(2,1)S(1)} %copy-done, ...), custom_call_target="tpu_custom_call" | custom-call | tf_op jit(solution)/shard_map/coarse/pallas_call | solution.py:342
  53.0 43.7 %tail.1 = (bf16[256,512]{1,0:T(8,128)(2,1)S(1)}, bf16[2,320,16,128]{3,2,1,0:T(8,128)(2,1)S(1)}) custom-call(f32[256,640]{1,0:T(8,128)S(1)} %get-tuple-element.14.ab_ref, bf16[256,512]{1,0:T(8,128)(2,1)S(1)} %copy-done.3, bf16[256,512]{1,0:T(8,128)(2,1)S(1)} %get-tuple-element.15.c_ref, bf16[256,512]{1,0:T(8,128)(2,1)S(1)} %copy-done, ...), custom_call_target="tpu_custom_call" | custom-call | tf_op jit(solution)/shard_map/tail/pallas_call | solution.py:620
  96.7 2.0 %unpack.1 = (bf16[256,512]{1,0:T(8,128)(2,1)}, bf16[256,256]{1,0:T(8,128)(2,1)}, bf16[256,512]{1,0:T(8,128)(2,1)}, bf16[512,1536]{1,0:T(8,128)(2,1)}, bf16[512,512]{1,0:T(8,128)(2,1)}) custom-call(bf16[256,512]{1,0:T(8,128)(2,1)S(1)} %get-tuple-element.21.out_ref, bf16[2,320,16,128]{3,2,1,0:T(8,128)(2,1)S(1)} %get-tuple-element.22.full), custom_call_target="tpu_custom_call" | custom-call | tf_op jit(solution)/shard_map/unpack/pallas_call | solution.py:646
Async XLA Ops:
  0.6 20.9 %copy-start = (bf16[256,512]{1,0:T(8,128)(2,1)S(1)}, bf16[256,512]{1,0:T(8,128)(2,1)}, u32[]{:S(2)}) copy-start(bf16[256,512]{1,0:T(8,128)(2,1)} %ct_ref.5) | copy-start | bytes 786436
  0.6 34.7 %copy-start.1 = (bf16[512,512]{1,0:T(8,128)(2,1)S(1)}, bf16[512,512]{1,0:T(8,128)(2,1)}, u32[]{:S(2)}) copy-start(bf16[512,512]{1,0:T(8,128)(2,1)} %ow_ref.3) | copy-start | bytes 1572868
  0.7 20.9 %copy-start.3 = (bf16[256,512]{1,0:T(8,128)(2,1)S(1)}, bf16[256,512]{1,0:T(8,128)(2,1)}, u32[]{:S(2)}) copy-start(bf16[256,512]{1,0:T(8,128)(2,1)} %pw_ref.3) | copy-start | bytes 786436
  0.7 34.7 %copy-start.2 = (bf16[512,1536]{1,0:T(8,128)(2,1)S(1)}, bf16[512,1536]{1,0:T(8,128)(2,1)}, u32[]{:S(2)}) copy-start(bf16[512,1536]{1,0:T(8,128)(2,1)} %w_ref.1) | copy-start | bytes 4718596
  1.5 1.0 %copy-start.4 = (bf16[1024,256]{1,0:T(8,128)(2,1)S(1)}, bf16[1024,256]{1,0:T(8,128)(2,1)}, u32[]{:S(2)}) copy-start(bf16[1024,256]{1,0:T(8,128)(2,1)} %x_hbm.1) | copy-start | bytes 1572868
  2.5 1.0 %copy-start.5 = (bf16[256,768]{1,0:T(8,128)(2,1)S(1)}, bf16[256,768]{1,0:T(8,128)(2,1)}, u32[]{:S(2)}) copy-start(bf16[256,768]{1,0:T(8,128)(2,1)} %w_hbm.1) | copy-start | bytes 1179652
  3.5 0.9 copy-start.6
  4.4 0.7 copy-start.7

commit v5 on v4

--- a/solution.py
+++ b/solution.py
@@ -157,7 +157,8 @@
             pltpu.VMEM((256, 256), BF),
             pltpu.SemaphoreType.DMA((4,)),
         ],
-        compiler_params=pltpu.CompilerParams(vmem_limit_bytes=24 * 1024 * 1024),
+        compiler_params=pltpu.CompilerParams(vmem_limit_bytes=54 * 1024 * 1024),
+        cost_estimate=pl.CostEstimate(flops=20 * 10**9, bytes_accessed=3 * 10**6, transcendentals=16 * 10**6),
         name="fine",
     )(count, offset, x, w, ow)
 
@@ -229,6 +230,7 @@
         compiler_params=pltpu.CompilerParams(
             collective_id=1, has_side_effects=True, vmem_limit_bytes=12 * 1024 * 1024
         ),
+        cost_estimate=pl.CostEstimate(flops=9 * 10**9, bytes_accessed=10**6, transcendentals=10**5),
         name="middle",
     )(ab, pw, ct)
 

time: 98.9 us -> 97.7 us (0.988)
  local copies, waits for them, and re-layouts: 3.64 us -> 1.13 us
  Pallas kernels: 93.5 us -> 95 us
    unnamed x16 -> x10, local copies, waits for them, and re-layouts: 3.64 us -> 1.13 us
    pallas_call x1, Pallas kernels: 16.4 us -> 18 us  [fine_call(): pl.pallas_call(fine_kernel, out_shape=jax.ShapeDtypeStruct((288, 640), F3...]
where the time goes in v5:
time: 97.7 us; the launch traced here: 97.5 us
  Pallas kernels  95 us (97%)
  between operations  1.36 us (1%)
  local copies, waits for them, and re-layouts  1.13 us (1%)
    pallas_call x1, Pallas kernels, tail_call(): pl.pallas_call(tail_kernel, out_shape=(jax.ShapeDtypeStruct((256, 512), B...  43.8 us
    pallas_call x1, Pallas kernels, fine_call(): pl.pallas_call(fine_kernel, out_shape=jax.ShapeDtypeStruct((288, 640), F3...  18 us
    pallas_call x1, Pallas kernels, coarse_call(): pl.pallas_call(coarse_kernel, out_shape=(jax.ShapeDtypeStruct((512, 512),...  17.7 us
    pallas_call x1, Pallas kernels, middle_call(): pl.pallas_call(middle_kernel, out_shape=(jax.ShapeDtypeStruct((256, 640),...  13.6 us
    pallas_call x1, Pallas kernels, unpack_call(): pl.pallas_call(unpack_kernel, out_shape=(jax.ShapeDtypeStruct((256, 512),...  1.97 us

profile of v5, /device:TPU:1, one launch (start us, length us, event | category | flops | bytes accessed | tf_op | source)
XLA Modules:
  0.0 97.5 jit_solution(5536846644296203575)
XLA Ops:
  1.3 0.0 copy-start.2
  1.3 0.0 copy-start.3
  1.3 18.0 %fine.1.ab_ref = f32[288,640]{1,0:T(8,128)} custom-call(s32[1]{0:T(128)S(6)} %copy.14.cnt_ref, s32[1,1024]{1,0:T(1,128)} %bitcast.1, bf16[1024,256]{1,0:T(8,128)(2,1)} %x_hbm.1, bf16[256,768]{1,0:T(8,128)(2,1)} %w_hbm.1, bf16[256,256]{1,0:T(8,128)(2,1)} %ow_hbm.1), custom_call_target="tpu_custom_call" | custom-call | flops 20000000000 | bytes 3000000 | tf_op jit(solution)/shard_map/fine/pallas_call | solution.py:144
  19.3 0.0 copy-done.2
  19.3 0.0 copy-done.3
  19.3 0.0 copy-start.4
  19.3 1.1 %copy-done.4 = f32[288,640]{1,0:T(8,128)S(1)} copy-done((f32[288,640]{1,0:T(8,128)S(1)}, f32[288,640]{1,0:T(8,128)}, u32[]{:S(2)}) %copy-start.4) | copy-done | bytes 737304
  20.4 0.0 copy-start
  20.4 0.0 copy-start.1
  20.4 13.6 %middle.1 = (f32[256,640]{1,0:T(8,128)S(1)}, bf16[256,512]{1,0:T(8,128)(2,1)S(1)}, bf16[256,512]{1,0:T(8,128)(2,1)S(1)}, bf16[256,512]{1,0:T(8,128)(2,1)S(1)}) custom-call(f32[288,640]{1,0:T(8,128)S(1)} %copy-done.4, bf16[256,512]{1,0:T(8,128)(2,1)S(1)} %copy-done.3, bf16[256,512]{1,0:T(8,128)(2,1)S(1)} %copy-done.2), custom_call_target="tpu_custom_call" | custom-call | flops 8999999488 | bytes 1000000 | tf_op jit(solution)/shard_map/middle/pallas_call | solution.py:220
  34.0 0.0 copy-done
  34.0 0.0 copy-done.1
  34.0 17.7 %coarse.1 = (bf16[512,512]{1,0:T(8,128)(2,1)S(1)}, bf16[512,256]{1,0:T(8,128)(2,1)S(1)}, bf16[256,16,128]{2,1,0:T(8,128)(2,1)S(1)}) custom-call(bf16[256,512]{1,0:T(8,128)(2,1)S(1)} %get-tuple-element.15.c_ref, bf16[256,512]{1,0:T(8,128)(2,1)S(1)} %get-tuple-element.16.cf_ref, bf16[256,512]{1,0:T(8,128)(2,1)S(1)} %copy-done.2, ...), custom_call_target="tpu_custom_call" | custom-call | tf_op jit(solution)/shard_map/coarse/pallas_call | solution.py:344
  51.7 43.8 %tail.1 = (bf16[256,512]{1,0:T(8,128)(2,1)S(1)}, bf16[2,320,16,128]{3,2,1,0:T(8,128)(2,1)S(1)}) custom-call(f32[256,640]{1,0:T(8,128)S(1)} %get-tuple-element.14.ab_ref, bf16[256,512]{1,0:T(8,128)(2,1)S(1)} %copy-done.3, bf16[256,512]{1,0:T(8,128)(2,1)S(1)} %get-tuple-element.15.c_ref, bf16[256,512]{1,0:T(8,128)(2,1)S(1)} %copy-done.2, ...), custom_call_target="tpu_custom_call" | custom-call | tf_op jit(solution)/shard_map/tail/pallas_call | solution.py:622
  95.5 2.0 %unpack.1 = (bf16[256,512]{1,0:T(8,128)(2,1)}, bf16[256,256]{1,0:T(8,128)(2,1)}, bf16[256,512]{1,0:T(8,128)(2,1)}, bf16[512,1536]{1,0:T(8,128)(2,1)}, bf16[512,512]{1,0:T(8,128)(2,1)}) custom-call(bf16[256,512]{1,0:T(8,128)(2,1)S(1)} %get-tuple-element.21.out_ref, bf16[2,320,16,128]{3,2,1,0:T(8,128)(2,1)S(1)} %get-tuple-element.22.full), custom_call_target="tpu_custom_call" | custom-call | tf_op jit(solution)/shard_map/unpack/pallas_call | solution.py:648
Async XLA Ops:
  1.3 18.0 %copy-start.2 = (bf16[256,512]{1,0:T(8,128)(2,1)S(1)}, bf16[256,512]{1,0:T(8,128)(2,1)}, u32[]{:S(2)}) copy-start(bf16[256,512]{1,0:T(8,128)(2,1)} %ct_ref.5) | copy-start | bytes 786436
  1.3 18.0 %copy-start.3 = (bf16[256,512]{1,0:T(8,128)(2,1)S(1)}, bf16[256,512]{1,0:T(8,128)(2,1)}, u32[]{:S(2)}) copy-start(bf16[256,512]{1,0:T(8,128)(2,1)} %pw_ref.3) | copy-start | bytes 786436
  19.3 1.1 %copy-start.4 = (f32[288,640]{1,0:T(8,128)S(1)}, f32[288,640]{1,0:T(8,128)}, u32[]{:S(2)}) copy-start(f32[288,640]{1,0:T(8,128)} %fine.1.ab_ref) | copy-start | bytes 2211844
  20.4 13.6 %copy-start = (bf16[512,512]{1,0:T(8,128)(2,1)S(1)}, bf16[512,512]{1,0:T(8,128)(2,1)}, u32[]{:S(2)}) copy-start(bf16[512,512]{1,0:T(8,128)(2,1)} %ow_ref.3) | copy-start | bytes 1572868
  20.4 13.6 %copy-start.1 = (bf16[512,1536]{1,0:T(8,128)(2,1)S(1)}, bf16[512,1536]{1,0:T(8,128)(2,1)}, u32[]{:S(2)}) copy-start(bf16[512,1536]{1,0:T(8,128)(2,1)} %w_ref.1) | copy-start | bytes 4718596
